TPU v7x, 32 devices: a whole 2x2x4 slice. The times are simulated.
32 devices in a mesh: exp: 8 (over z, x), head: 4 (over y, core).
Axes of the slice: x: 2, y: 2, z: 4, core: 2. Of those that a mesh axis runs over, the one named last changes fastest.
Arguments:
- normed_input: bfloat16 [8, 32, 4096], P('exp', None, 'head'), may hold values from -11 to 11
- norm_gain: float32 [4096], P('head'), may hold values from 0.5 to 1.5
- norm_scale: float32 [8, 32], P('exp'), may hold values from 0.4 to 4
- out_grad: bfloat16 [8, 32, 4096], P('exp', None, 'head'), may hold values from -6 to 6
- router_weight: bfloat16 [4096, 16], P('head'), may hold values from -0.125 to 0.125
- routed_experts: int32 [8, 32, 8], P('exp'), may hold values from 0 to 15, all different within a row; in each aligned block of 32 rows (0 to 31, 32 to 63, ..., all dimensions but the last counted through in order) at most 30 rows name the same one
- expert_grad: bfloat16 [16, 8, 30, 4096], P('exp', None, None, 'head'), may hold values from -10 to 10, as said below
- gate_grad: bfloat16 [16, 8, 30], P('exp'), may hold values from -48 to 48
- out_proj: bfloat16 [8192, 4096], P('head'), may hold values from -0.0625 to 0.0625
- query_states: bfloat16 [8, 32, 8192], P('exp', None, 'head'), may hold values from -5 to 5
- rotated_keys: bfloat16 [8, 32, 512], P('exp'), may hold values from -5 to 5
- value_tensor: bfloat16 [8, 32, 512], P('exp'), may hold values from -6 to 6
Outputs:
- grad_hidden: bfloat16 [8, 32, 4096], P('exp', None, 'head')
- grad_query: bfloat16 [8, 32, 8192], P('exp', 'head')
- key_gradient: bfloat16 [8, 32, 512], P('exp', 'head')
- value_gradient: bfloat16 [8, 32, 512], P('exp', 'head')
Inputs may be any that keep to these rules, and one draw needn't show every extreme that they name: `routed_experts`: each token names 8 different experts. Within one sequence, an aligned block of 32 rows, no expert is named by more than 30 tokens, a bound that some block reaches. `expert_grad`: slot c of expert e for sequence s holds the row of the c-th token of sequence s, in order of position, that names e; slots past that count hold unrelated values. `gate_grad`: same slot layout as expert_grad.
All inputs are finite; a program needn't handle non-finite values.
Results may differ from a plain program's by a relative error of at most 0.01225.
Values may be sent and summed in bfloat16 or wider, within the bound.
A program may use at most 64 MiB of HBM per device.

v0:
```python
import functools
import math

import jax
import jax.numpy as jnp
from jax import lax
from jax.experimental import pallas as pl
from jax.experimental.pallas import tpu as pltpu
from jax.sharding import PartitionSpec as P

QUERY_HEADS = 64
KEY_VALUE_HEADS = 4
HEAD_WIDTH = 128
MESH = pl.DeviceIdType.MESH
NT = (((1,), (1,)), ((), ()))
TN = (((0,), (0,)), ((), ()))
F32 = jnp.float32
BF16 = jnp.bfloat16


def mm(a, b, dims=(((1,), (0,)), ((), ()))):
    return lax.dot_general(a, b, dims, preferred_element_type=F32)


def kernel(
    n_exp, n_head, width_total,
    x_hbm, gain_hbm, scale_hbm, og_hbm, router_hbm, ids_hbm, expert_hbm, gg_hbm, proj_ref,
    q_hbm, k_hbm, v_hbm,
    gh_out, gq_out, gk_out, gv_out,
    x_ref, gain_ref, scale_ref, og_ref, router_ref, ids_ref, expert_ref, gg_ref,
    q_ref, k_ref, v_ref, in_sem,
    w_v, row_send, rows, gg_in, logit, gt, gates, p_out, p_in, sg_out, sg_in, diff_v, inner_v, gh_all, x_all,
    ctx, probs_v, q_send, q_in, k_send, k_in, v_send, v_in,
    w_sem, xs, xr, ggs, ggr, ls, lr, gs, gr, ps, pr, ss, sr, ins, inr, hs, hr, xas, xar,
    qs, qr, ks, kr, vs, vr,
):
    e = lax.axis_index("exp")
    h = lax.axis_index("head")
    x = lax.rem(e, 2)
    z = e // 2
    cols = n_exp // 2
    seq, width = x_ref.shape
    experts_all = router_ref.shape[0]
    local, cap = expert_ref.shape[:2]
    room = rows.shape[2] // local
    pair = 2 * local
    heads = proj_ref.shape[0] // HEAD_WIDTH
    tok = seq // n_head
    partner = 2 * z + 1 - x

    def exp_peer(i):
        return {"exp": 2 * i + x}

    def send(src, dst, s_sem, r_sem, to):
        return pltpu.make_async_remote_copy(
            src_ref=src, dst_ref=dst, send_sem=s_sem, recv_sem=r_sem,
            device_id=to, device_id_type=MESH,
        )

    chips = n_head // 2
    chip, core = h // 2, lax.rem(h, 2)
    head_peers = [2 * chip + 1 - core]
    for i in range(1, chips):
        there = 2 * lax.rem(chip + i, chips)
        head_peers += [there + core, there + 1 - core]
    col_peers = [lax.rem(z + i, cols) for i in range(1, cols)]

    barrier = pltpu.get_barrier_semaphore()
    pl.semaphore_signal(barrier, inc=1, device_id={"exp": partner}, device_id_type=MESH)
    for p in col_peers:
        pl.semaphore_signal(barrier, inc=1, device_id=exp_peer(p), device_id_type=MESH)
    for p in head_peers:
        pl.semaphore_signal(barrier, inc=1, device_id={"head": p}, device_id_type=MESH)

    w_copies = []
    for j in range(n_head):
        w_copies.append(
            pltpu.make_async_copy(
                proj_ref.at[:, pl.ds(j * width, width)], w_v.at[j], w_sem.at[j]
            )
        )
    loads = [
        pltpu.make_async_copy(src, dst, in_sem.at[i])
        for i, (src, dst) in enumerate((
            (expert_hbm, expert_ref), (x_hbm, x_ref), (gain_hbm, gain_ref),
            (router_hbm, router_ref), (ids_hbm, ids_ref), (gg_hbm, gg_ref),
            (q_hbm, q_ref), (k_hbm, k_ref), (v_hbm, v_ref), (og_hbm, og_ref),
            (scale_hbm, scale_ref),
        ))
    ]
    for cp in loads + w_copies:
        cp.start()

    loads[0].wait()
    flat = expert_ref.reshape(local, cap * n_exp, width)

    def pick(c_list, side):
        m = len(c_list) * room
        r_i = lax.broadcasted_iota(jnp.int32, (m, cap * n_exp), 0)
        k_i = lax.broadcasted_iota(jnp.int32, (m, cap * n_exp), 1)
        group = r_i // room
        number = jnp.zeros_like(r_i)
        for i, c in enumerate(c_list):
            number = jnp.where(group == i, 2 * c + side, number)
        slot = r_i - group * room
        one = jnp.logical_and(slot < cap, slot * n_exp + number == k_i)
        return jnp.where(one, 1.0, 0.0).astype(BF16)

    def row_copy(c):
        return send(row_send.at[c], rows.at[c, x], xs.at[c], xr.at[c], {"exp": partner})

    def row_wait(c):
        return send(row_send.at[c], rows.at[c, 1 - x], xs.at[c], xr.at[c], {"exp": partner})

    all_cols = col_peers + [z]
    step = min(cols, 4)
    for first in range(0, cols, step):
        some = all_cols[first : first + step]
        chosen = pick(some, 1 - x)
        for j in range(local):
            got = mm(chosen, flat[j]).astype(BF16)
            for i, c in enumerate(some):
                row_send[c, j * room : (j + 1) * room] = got[i * room : (i + 1) * room]
    pl.semaphore_wait(barrier, 1 + (cols - 1) + (n_head - 1))

    loads[5].wait()
    gg_copy = send(gg_ref, gg_in, ggs, ggr, {"exp": partner})
    gg_copy.start()
    for c in all_cols:
        row_copy(c).start()

    for cp in loads[1:5]:
        cp.wait()
    hidden = x_ref[...].astype(F32)
    gain = gain_ref[...]
    scaled = hidden * gain
    x_all[h] = x_ref[...]
    logit[h] = mm(router_ref[...], scaled.astype(BF16), NT)

    def wide_copy(buf, src, to, s_sem, r_sem):
        return send(buf.at[src], buf.at[src], s_sem.at[to], r_sem.at[src], {"head": to})

    def logit_copy(src, to):
        return send(logit.at[src], logit.at[src], ls.at[to], lr.at[src], {"head": to})

    for p in head_peers:
        logit_copy(h, p).start()
    for p in head_peers:
        wide_copy(x_all, h, p, xas, xar).start()


    for first in range(0, cols, step):
        some = all_cols[first : first + step]
        chosen = pick(some, x)
        for j in range(local):
            got = mm(chosen, flat[j]).astype(BF16)
            for i, c in enumerate(some):
                rows[c, x, j * room : (j + 1) * room] = got[i * room : (i + 1) * room]

    expert_i = lax.broadcasted_iota(jnp.int32, (experts_all, seq), 0)
    member = ids_ref[0:1] == expert_i
    for i in range(1, ids_ref.shape[0]):
        member = jnp.logical_or(member, ids_ref[i : i + 1] == expert_i)
    row_i = lax.broadcasted_iota(jnp.int32, (seq, seq), 0)
    col_i = lax.broadcasted_iota(jnp.int32, (seq, seq), 1)

    for p in head_peers:
        logit_copy(p, p).wait_recv()
    total = logit[0]
    for i in range(1, n_head):
        total = total + logit[i]
    total = jnp.where(member, total, -jnp.inf)
    top = jnp.max(total, axis=0, keepdims=True)
    weights = jnp.exp(total - top)
    weights = weights / jnp.sum(weights, axis=0, keepdims=True)
    weights_t = jnp.where(member, weights, -1.0)
    for c in range(cols):
        gt[c] = weights_t[c * pair : (c + 1) * pair]

    def gate_copy(c):
        return send(gt.at[c], gates.at[z], gs.at[c], gr.at[z], exp_peer(c))

    def gate_wait(c):
        return send(gt.at[c], gates.at[c], gs.at[c], gr.at[c], exp_peer(c))

    for c in col_peers:
        gate_copy(c).start()

    for cp in loads[6:]:
        cp.wait()
    kv = h * heads // (QUERY_HEADS // KEY_VALUE_HEADS)
    lanes = pl.ds(pl.multiple_of(kv * HEAD_WIDTH, HEAD_WIDTH), HEAD_WIDTH)
    key_block = k_ref[:, lanes]
    value_block = v_ref[:, lanes]

    def stacked(a):
        return jnp.concatenate(
            [a[:, i * HEAD_WIDTH : (i + 1) * HEAD_WIDTH] for i in range(heads)], axis=0
        )

    inv_sqrt = 1.0 / math.sqrt(HEAD_WIDTH)
    queries = stacked(q_ref[...])
    scores = mm(queries, key_block, NT) * inv_sqrt
    position = lax.rem(lax.broadcasted_iota(jnp.int32, scores.shape, 0), seq)
    causal = position >= lax.broadcasted_iota(jnp.int32, scores.shape, 1)
    scores = jnp.where(causal, scores, -jnp.inf)
    probs = jnp.exp(scores - jnp.max(scores, axis=1, keepdims=True))
    probs_v[...] = probs / jnp.sum(probs, axis=1, keepdims=True)

    earlier = (row_i < col_i).astype(BF16)
    slot_i = lax.broadcasted_iota(jnp.int32, (room, seq), 0)
    seq_i = lax.broadcasted_iota(jnp.int32, (n_exp, seq), 0)
    gg_copy.wait_recv()

    def contribution(c, w):
        named = w >= 0.0
        before = mm(jnp.where(named, 1.0, 0.0).astype(BF16), earlier).astype(jnp.int32)
        slot_grads = []
        spread = []
        for j in range(pair):
            hit = jnp.logical_and(before[j : j + 1] == slot_i, named[j : j + 1])
            spread.append(jnp.where(hit, w[j : j + 1], 0.0).astype(BF16))
            own_g = gg_ref[j % local].astype(F32)
            far_g = gg_in[j % local].astype(F32)
            table = jnp.where(x == j // local, own_g, far_g).astype(BF16)
            by_seq = mm(table, jnp.where(hit[:cap], 1.0, 0.0).astype(BF16))
            slot_grads.append(
                jnp.sum(jnp.where(seq_i == 2 * c + x, by_seq, 0.0), axis=0, keepdims=True)
            )
        out = mm(
            jnp.concatenate(spread, axis=0), rows[c].reshape(pair * room, width), TN
        )
        return out, slot_grads

    def part_copy(c):
        return send(p_out.at[c], p_in.at[z], ps.at[c], pr.at[z], exp_peer(c))

    def part_wait(c):
        return send(p_out.at[c], p_in.at[c], ps.at[c], pr.at[c], exp_peer(c))

    def slot_copy(c):
        return send(sg_out.at[c], sg_in.at[z], ss.at[c], sr.at[z], exp_peer(c))

    def slot_wait(c):
        return send(sg_out.at[c], sg_in.at[c], ss.at[c], sr.at[c], exp_peer(c))

    for c in col_peers:
        gate_wait(c).wait_recv()
        row_wait(c).wait_recv()
        out, slot_grads = contribution(c, gates[c])
        for j in range(pair):
            sg_out[c, j : j + 1] = slot_grads[j]
        p_out[c] = out.astype(BF16)
        slot_copy(c).start()
        part_copy(c).start()
    row_wait(z).wait_recv()
    grad, slot_grads = contribution(z, gt[z])
    for j in range(pair):
        sg_in[z, j : j + 1] = slot_grads[j]
    for c in col_peers:
        slot_wait(c).wait_recv()
    mean = jnp.zeros((1, seq), F32)
    for c in range(cols):
        mean = mean + jnp.sum(jnp.maximum(gt[c], 0.0) * sg_in[c], axis=0, keepdims=True)
    for c in range(cols):
        diff_v[c * pair : (c + 1) * pair] = jnp.maximum(gt[c], 0.0) * (sg_in[c] - mean)
    diff = diff_v[...]
    diff_hi = diff.astype(BF16)
    diff_lo = (diff - diff_hi.astype(F32)).astype(BF16)
    grad = grad + mm(diff_hi, router_ref[...], TN) + mm(diff_lo, router_ref[...], TN)
    for c in col_peers:
        part_wait(c).wait_recv()
        grad = grad + p_in[c].astype(F32)

    scale = jnp.sum(
        jnp.where(row_i == col_i, jnp.broadcast_to(scale_ref[...], (seq, seq)), 0.0),
        axis=1, keepdims=True,
    )
    base = og_ref[...].astype(F32) + scale * (gain * grad)
    gh_all[h] = base.astype(BF16)
    for p in head_peers:
        wide_copy(gh_all, h, p, hs, hr).start()
    inner_v[h] = jnp.broadcast_to(
        jnp.sum(scaled * grad, axis=1, keepdims=True), (seq, HEAD_WIDTH)
    )

    def inner_copy(src, to):
        return send(inner_v.at[src], inner_v.at[src], ins.at[to], inr.at[src], {"head": to})

    for p in head_peers:
        inner_copy(h, p).start()
    for cp in w_copies:
        cp.wait()

    rows_w = w_v.shape[1]
    tile = min(512, rows_w)
    for i, p in enumerate([h] + head_peers):
        if i:
            wide_copy(x_all, p, p, xas, xar).wait_recv()
            wide_copy(gh_all, p, p, hs, hr).wait_recv()
        a = jnp.concatenate([gh_all[p], x_all[p]], axis=0)
        for r in range(0, rows_w, tile):
            part = mm(a, w_v[p, r : r + tile], NT)
            if i:
                part = ctx[:, r : r + tile] + part
            ctx[:, r : r + tile] = part

    for p in head_peers:
        inner_copy(p, p).wait_recv()
    inner = inner_v[0]
    for i in range(1, n_head):
        inner = inner + inner_v[i]
    taken = scale * inner[:, 0:1] / width_total
    gh_out[...] = (base - hidden * taken).astype(BF16)

    ctx_s = stacked((ctx[:seq] - taken * ctx[seq:]).astype(BF16))
    probs = probs_v[...]
    prob_grads = mm(ctx_s, value_block, NT)
    delta = jnp.sum(probs * prob_grads, axis=1, keepdims=True)
    score_grads = (probs * (prob_grads - delta) * inv_sqrt).astype(BF16)
    gq = mm(score_grads, key_block)
    for d in range(n_head):
        for i in range(heads):
            r = i * seq + d * tok
            q_send[d, :, i * HEAD_WIDTH : (i + 1) * HEAD_WIDTH] = gq[r : r + tok].astype(BF16)

    def out_copy(buf, into, s_sem, r_sem, to):
        return send(buf.at[to], into.at[h], s_sem.at[to], r_sem.at[h], {"head": to})

    def out_wait(buf, into, s_sem, r_sem, src):
        return send(buf.at[src], into.at[src], s_sem.at[src], r_sem.at[src], {"head": src})

    for p in head_peers:
        out_copy(q_send, q_in, qs, qr, p).start()
    gk = mm(score_grads, queries, TN)
    gv = mm(probs.astype(BF16), ctx_s, TN)
    for d in range(n_head):
        k_send[d] = gk[d * tok : (d + 1) * tok].astype(BF16)
        v_send[d] = gv[d * tok : (d + 1) * tok].astype(BF16)
    for p in head_peers:
        out_copy(k_send, k_in, ks, kr, p).start()
        out_copy(v_send, v_in, vs, vr, p).start()
    q_in[h] = q_send[h]
    k_in[h] = k_send[h]
    v_in[h] = v_send[h]
    for p in head_peers:
        out_wait(q_send, q_in, qs, qr, p).wait_recv()
        out_wait(k_send, k_in, ks, kr, p).wait_recv()
        out_wait(v_send, v_in, vs, vr, p).wait_recv()
    span = heads * HEAD_WIDTH
    for i in range(n_head):
        gq_out[:, i * span : (i + 1) * span] = q_in[i]
    replicas = n_head // KEY_VALUE_HEADS
    for g in range(KEY_VALUE_HEADS):
        sum_k = k_in[g * replicas].astype(F32)
        sum_v = v_in[g * replicas].astype(F32)
        for i in range(1, replicas):
            sum_k = sum_k + k_in[g * replicas + i].astype(F32)
            sum_v = sum_v + v_in[g * replicas + i].astype(F32)
        gk_out[:, g * HEAD_WIDTH : (g + 1) * HEAD_WIDTH] = sum_k.astype(BF16)
        gv_out[:, g * HEAD_WIDTH : (g + 1) * HEAD_WIDTH] = sum_v.astype(BF16)

    gg_copy.wait_send()
    row_copy(z).wait_send()
    for c in col_peers:
        row_copy(c).wait_send()
        gate_copy(c).wait_send()
        slot_copy(c).wait_send()
        part_copy(c).wait_send()
    for p in head_peers:
        logit_copy(h, p).wait_send()
        inner_copy(h, p).wait_send()
        wide_copy(gh_all, h, p, hs, hr).wait_send()
        wide_copy(x_all, h, p, xas, xar).wait_send()
        out_copy(q_send, q_in, qs, qr, p).wait_send()
        out_copy(k_send, k_in, ks, kr, p).wait_send()
        out_copy(v_send, v_in, vs, vr, p).wait_send()


def write_out(*refs):
    n = (len(refs) - 1) // 2
    sems = refs[-1]
    copies = [
        pltpu.make_async_copy(refs[i], refs[n + i], sems.at[i]) for i in range(n)
    ]
    for cp in copies:
        cp.start()
    for cp in copies:
        cp.wait()


def solution(mesh):
    n_exp = mesh.shape["exp"]
    n_head = mesh.shape["head"]
    cols = n_exp // 2

    def per_device(
        normed_input, norm_gain, norm_scale, out_grad, router_weight, routed_experts,
        expert_grad, gate_grad, out_proj, query_states, rotated_keys, value_tensor,
    ):
        _, seq, width = normed_input.shape
        experts_all = router_weight.shape[1]
        local, _, cap, _ = expert_grad.shape
        pair = 2 * local
        span, width_total = out_proj.shape
        heads = span // HEAD_WIDTH
        tok = seq // n_head
        kv_width = rotated_keys.shape[2]
        vm = pltpu.VMEM
        dma = pltpu.SemaphoreType.DMA
        vmem = pl.BlockSpec(memory_space=pltpu.VMEM)
        hbm = pl.BlockSpec(memory_space=pltpu.HBM)
        room = -(-cap // 16) * 16
        top_k = routed_experts.shape[2]
        outs = pl.pallas_call(
            functools.partial(kernel, n_exp, n_head, width_total),
            name="moe_attention_backward",
            out_shape=(
                jax.ShapeDtypeStruct((seq, width), BF16),
                jax.ShapeDtypeStruct((tok, n_head * span), BF16),
                jax.ShapeDtypeStruct((tok, kv_width), BF16),
                jax.ShapeDtypeStruct((tok, kv_width), BF16),
            ),
            in_specs=[hbm] * 12,
            out_specs=(vmem,) * 4,
            scratch_shapes=[
                vm((seq, width), BF16), vm((1, width), F32), vm((1, seq), F32),
                vm((seq, width), BF16), vm((experts_all, width), BF16),
                vm((top_k, seq), jnp.int32), vm((local, cap, n_exp, width), BF16),
                vm(gate_grad.shape, BF16), vm((seq, span), BF16),
                vm((seq, kv_width), BF16), vm((seq, kv_width), BF16), dma((11,)),
                vm((n_head, span, width), BF16),
                vm((cols, local * room, width), BF16),
                vm((cols, 2, local * room, width), BF16),
                vm(gate_grad.shape, BF16),
                vm((n_head, experts_all, seq), F32),
                vm((cols, pair, seq), F32),
                vm((cols, pair, seq), F32),
                vm((cols, seq, width), BF16),
                vm((cols, seq, width), BF16),
                vm((cols, pair, seq), F32),
                vm((cols, pair, seq), F32),
                vm((experts_all, seq), F32),
                vm((n_head, seq, HEAD_WIDTH), F32),
                vm((n_head, seq, width), BF16),
                vm((n_head, seq, width), BF16),
                vm((2 * seq, span), F32),
                vm((heads * seq, seq), F32),
                vm((n_head, tok, span), BF16),
                vm((n_head, tok, span), BF16),
                vm((n_head, tok, HEAD_WIDTH), BF16),
                vm((n_head, tok, HEAD_WIDTH), BF16),
                vm((n_head, tok, HEAD_WIDTH), BF16),
                vm((n_head, tok, HEAD_WIDTH), BF16),
                dma((n_head,)), dma((cols,)), dma((cols,)), dma, dma,
                dma((n_head,)), dma((n_head,)), dma((cols,)), dma((cols,)),
                dma((cols,)), dma((cols,)), dma((cols,)), dma((cols,)),
                dma((n_head,)), dma((n_head,)), dma((n_head,)), dma((n_head,)),
                dma((n_head,)), dma((n_head,)), dma((n_head,)), dma((n_head,)),
                dma((n_head,)), dma((n_head,)), dma((n_head,)), dma((n_head,)),
            ],
            compiler_params=pltpu.CompilerParams(
                collective_id=0, has_side_effects=True, vmem_limit_bytes=48 * 1024 * 1024
            ),
        )(
            *(
                pltpu.with_memory_space_constraint(a, pltpu.HBM)
                for a in (
                    normed_input[0], norm_gain[None], norm_scale, out_grad[0], router_weight.T,
                    routed_experts[0].T, jnp.transpose(expert_grad, (0, 2, 1, 3)), gate_grad,
                    out_proj, query_states[0], rotated_keys[0], value_tensor[0],
                )
            )
        )
        outs = pl.pallas_call(
            write_out,
            name="write_out",
            out_shape=tuple(jax.ShapeDtypeStruct(o.shape, o.dtype) for o in outs),
            in_specs=[vmem] * 4,
            out_specs=(hbm,) * 4,
            scratch_shapes=[dma((4,))],
            compiler_params=pltpu.CompilerParams(vmem_limit_bytes=1024 * 1024),
        )(*outs)
        return tuple(o[None] for o in outs)

    placed = (
        P("exp", None, "head"),
        P("head"),
        P("exp", None),
        P("exp", None, "head"),
        P("head", None),
        P("exp", None, None),
        P("exp", None, None, "head"),
        P("exp", None, None),
        P("head", None),
        P("exp", None, "head"),
        P("exp", None, None),
        P("exp", None, None),
    )
    return jax.shard_map(
        per_device,
        mesh=mesh,
        in_specs=placed,
        out_specs=(
            P("exp", None, "head"),
            P("exp", "head", None),
            P("exp", "head", None),
            P("exp", "head", None),
        ),
        check_vma=False,
    )
```

profile of v0, /device:TPU:0, one launch (start us, length us, event | category | flops | bytes accessed | tf_op | source)
XLA Modules:
  0.0 32.1 jit_solution(12092649387698587379)
XLA Ops:
  0.6 30.7 %moe_attention_backward.1 = (bf16[32,1024]{1,0:T(8,128)(2,1)S(1)}, bf16[8,8192]{1,0:T(8,128)(2,1)S(1)}, bf16[8,512]{1,0:T(8,128)(2,1)S(1)}, bf16[8,512]{1,0:T(8,128)(2,1)S(1)}) custom-call(bf16[32,1024]{1,0:T(8,128)(2,1)} %bitcast.17, f32[1,1024]{1,0:T(1,128)} %bitcast.22, f32[1,32]{1,0:T(1,128)} %scale_hbm.1, bf16[32,1024]{1,0:T(8,128)(2,1)} %bitcast.18, ...), custom_call_target="tpu_custom_call" | custom-call | tf_op jit(solution)/shard_map/moe_attention_backward/pallas_call | solution.py:415
  31.3 0.7 %write_out.1 = (bf16[32,1024]{1,0:T(8,128)(2,1)}, bf16[8,8192]{1,0:T(8,128)(2,1)}, bf16[8,512]{1,0:T(8,128)(2,1)}, bf16[8,512]{1,0:T(8,128)(2,1)}) custom-call(bf16[32,1024]{1,0:T(8,128)(2,1)S(1)} %get-tuple-element.12.refs_0_, bf16[8,8192]{1,0:T(8,128)(2,1)S(1)} %get-tuple-element.13.refs_1_, bf16[8,512]{1,0:T(8,128)(2,1)S(1)} %get-tuple-element.14.refs_2_, ...), custom_call_target="tpu_custom_call" | custom-call | tf_op jit(solution)/shard_map/write_out/pallas_call | solution.py:475
where the time goes:
time: 32.2 us; the launch traced here: 32.1 us
  Pallas kernels  31.4 us (98%)
  between operations  0.64 us (2%)
    pallas_call x1, Pallas kernels, per_device(): pl.pallas_call(functools.partial(kernel, n_exp, n_head, width_total), nam...  30.7 us
    pallas_call x1, Pallas kernels, per_device(): pl.pallas_call(write_out, name='write_out', out_shape=tuple((jax.ShapeDty...  0.72 us

commit v1 on v0

v1 whole, which is shorter than its diff:
```python
import functools
import math

import jax
import jax.numpy as jnp
from jax import lax
from jax.experimental import pallas as pl
from jax.experimental.pallas import tpu as pltpu
from jax.sharding import PartitionSpec as P

QUERY_HEADS = 64
KEY_VALUE_HEADS = 4
HEAD_WIDTH = 128
MESH = pl.DeviceIdType.MESH
NT = (((1,), (1,)), ((), ()))
TN = (((0,), (0,)), ((), ()))
F32 = jnp.float32
BF16 = jnp.bfloat16


def mm(a, b, dims=(((1,), (0,)), ((), ()))):
    return lax.dot_general(a, b, dims, preferred_element_type=F32)


def kernel(
    n_exp, n_head, width_total,
    x_hbm, gain_hbm, scale_hbm, og_hbm, router_hbm, ids_hbm, expert_hbm, gg_hbm, proj_ref,
    q_hbm, k_hbm, v_hbm,
    gh_out, gq_out, gk_out, gv_out,
    gain_ref, scale_ref, og_ref, router_ref, ids_ref, expert_ref, gg_ref,
    q_ref, k_ref, v_ref, in_sem,
    w_v, row_send, rows, gg_in, logit, gt, gates, p_out, p_in, sg_out, sg_in, diff_v, inner_v, gh_all, x_all,
    ctx, probs_v, q_send, q_in, kv_send, kv_in,
    w_sem, send_sem, xr, ggr, lr, gr, pr, sr, inr, hr, xar, qr, kvr, up_sem, down_sem,
):
    e = lax.axis_index("exp")
    h = lax.axis_index("head")
    x = lax.rem(e, 2)
    z = e // 2
    cols = n_exp // 2
    seq, width = x_all.shape[1:]
    experts_all = router_ref.shape[0]
    local, cap = expert_ref.shape[:2]
    room = rows.shape[2] // local
    pair = 2 * local
    heads = proj_ref.shape[0] // HEAD_WIDTH
    tok = seq // n_head
    half = width // 2
    partner = 2 * z + 1 - x
    ROWS, GG, LOGIT, GATE, PART, SLOT, GH, INNER, XALL, QS, KVS = range(11)

    def exp_peer(i):
        return {"exp": 2 * i + x}

    def send(src, dst, s_sem, r_sem, to):
        return pltpu.make_async_remote_copy(
            src_ref=src, dst_ref=dst, send_sem=send_sem.at[s_sem], recv_sem=r_sem,
            device_id=to, device_id_type=MESH,
        )

    def drain(ref, sem):
        pltpu.make_async_copy(ref, ref, sem).wait()

    chips = n_head // 2
    chip, core = h // 2, lax.rem(h, 2)
    sibling = 2 * chip + 1 - core
    same, cross = [], []
    for i in range(1, chips):
        there = 2 * lax.rem(chip + i, chips)
        same.append(there + core)
        cross.append(there + 1 - core)
    head_peers = [sibling] + same + cross
    if cols == 4:
        col_peers = [3 * (1 - z // 2), 2 - z // 2, z + 1 - 2 * lax.rem(z, 2)]
    else:
        col_peers = [lax.rem(z + i, cols) for i in range(1, cols)]
    all_cols = col_peers + [z]

    barrier = pltpu.get_barrier_semaphore()
    pl.semaphore_signal(barrier, inc=1, device_id={"exp": partner}, device_id_type=MESH)
    for p in head_peers:
        pl.semaphore_signal(barrier, inc=1, device_id={"head": p}, device_id_type=MESH)

    @pl.when(z > 0)
    def _():
        pl.semaphore_signal(barrier, inc=1, device_id=exp_peer(z - 1), device_id_type=MESH)

    @pl.when(z < cols - 1)
    def _():
        pl.semaphore_signal(barrier, inc=1, device_id=exp_peer(z + 1), device_id_type=MESH)

    greeted = 1 + (n_head - 1) + (z + cols - 1) // cols + (2 * cols - 2 - z) // cols

    loads = {}
    for i, (name, src, dst) in enumerate((
        ("x", x_hbm, x_all.at[h]), ("gain", gain_hbm, gain_ref), ("router", router_hbm, router_ref),
        ("expert", expert_hbm, expert_ref), ("gg", gg_hbm, gg_ref), ("ids", ids_hbm, ids_ref),
        ("q", q_hbm, q_ref), ("k", k_hbm, k_ref), ("v", v_hbm, v_ref), ("og", og_hbm, og_ref),
        ("scale", scale_hbm, scale_ref),
    )):
        loads[name] = pltpu.make_async_copy(src, dst, in_sem.at[i])
    for cp in loads.values():
        cp.start()
    w_copies = [
        pltpu.make_async_copy(proj_ref.at[:, pl.ds(j * width, width)], w_v.at[j], w_sem)
        for j in range(n_head)
    ]

    for name in ("x", "gain", "router"):
        loads[name].wait()
    gain = gain_ref[...]

    def hidden_f32():
        return x_all[h].astype(F32)

    logit[h] = mm(router_ref[...], (hidden_f32() * gain).astype(BF16), NT)
    pl.semaphore_wait(barrier, greeted)

    def logit_copy(src, to):
        return send(logit.at[src], logit.at[src], LOGIT, lr, {"head": to})

    def x_copy(src, to):
        return send(x_all.at[src], x_all.at[src], XALL, xar, {"head": to})

    for p in head_peers:
        logit_copy(h, p).start()

    if cols > 2:
        @pl.when(z == 1)
        def _():
            pl.semaphore_signal(up_sem, inc=1, device_id=exp_peer(z + 1), device_id_type=MESH)

        @pl.when(z == cols - 2)
        def _():
            pl.semaphore_signal(down_sem, inc=1, device_id=exp_peer(z - 1), device_id_type=MESH)

    for p in head_peers:
        x_copy(h, p).start()
    loads["gg"].wait()
    gg_copy = send(gg_ref, gg_in, GG, ggr, {"exp": partner})
    gg_copy.start()

    loads["expert"].wait()
    for cp in w_copies:
        cp.start()
    flat = expert_ref.reshape(local, cap * n_exp, width)

    def pick(c_list, side):
        m = len(c_list) * room
        r_i = lax.broadcasted_iota(jnp.int32, (m, cap * n_exp), 0)
        k_i = lax.broadcasted_iota(jnp.int32, (m, cap * n_exp), 1)
        group = r_i // room
        number = jnp.zeros_like(r_i)
        for i, c in enumerate(c_list):
            number = jnp.where(group == i, 2 * c + side, number)
        slot = r_i - group * room
        one = jnp.logical_and(slot < cap, slot * n_exp + number == k_i)
        return jnp.where(one, 1.0, 0.0).astype(BF16)

    def row_copy(c, j):
        part = pl.ds(j * room, room)
        return send(row_send.at[c, part], rows.at[c, x, part], ROWS, xr.at[c], {"exp": partner})

    step = min(cols, 4)
    for first in range(0, cols, step):
        some = all_cols[first : first + step]
        chosen = pick(some, 1 - x)
        for j in range(local):
            got = mm(chosen, flat[j]).astype(BF16)
            for i, c in enumerate(some):
                row_send[c, j * room : (j + 1) * room] = got[i * room : (i + 1) * room]
            row_copy(some[0], j).start()
        for c in some[1:]:
            for j in range(local):
                row_copy(c, j).start()

    for first in range(0, cols, step):
        some = all_cols[first : first + step]
        chosen = pick(some, x)
        for j in range(local):
            got = mm(chosen, flat[j]).astype(BF16)
            for i, c in enumerate(some):
                rows[c, x, j * room : (j + 1) * room] = got[i * room : (i + 1) * room]

    if cols > 3:
        @pl.when(jnp.logical_and(z > 1, z < cols - 1))
        def _():
            pl.semaphore_wait(up_sem, 1)
            pl.semaphore_signal(up_sem, inc=1, device_id=exp_peer(z + 1), device_id_type=MESH)

        @pl.when(jnp.logical_and(z > 0, z < cols - 2))
        def _():
            pl.semaphore_wait(down_sem, 1)
            pl.semaphore_signal(down_sem, inc=1, device_id=exp_peer(z - 1), device_id_type=MESH)

    for name in ("ids", "q", "k", "v"):
        loads[name].wait()
    kv = h * heads // (QUERY_HEADS // KEY_VALUE_HEADS)
    lanes = pl.ds(pl.multiple_of(kv * HEAD_WIDTH, HEAD_WIDTH), HEAD_WIDTH)

    def stacked(a):
        return jnp.concatenate(
            [a[:, i * HEAD_WIDTH : (i + 1) * HEAD_WIDTH] for i in range(a.shape[1] // HEAD_WIDTH)],
            axis=0,
        )

    inv_sqrt = 1.0 / math.sqrt(HEAD_WIDTH)
    scores = mm(stacked(q_ref[...]), k_ref[:, lanes], NT) * inv_sqrt
    position = lax.rem(lax.broadcasted_iota(jnp.int32, scores.shape, 0), seq)
    causal = position >= lax.broadcasted_iota(jnp.int32, scores.shape, 1)
    scores = jnp.where(causal, scores, -jnp.inf)
    probs = jnp.exp(scores - jnp.max(scores, axis=1, keepdims=True))
    probs_v[...] = probs / jnp.sum(probs, axis=1, keepdims=True)

    expert_i = lax.broadcasted_iota(jnp.int32, (experts_all, seq), 0)
    member = ids_ref[0:1] == expert_i
    for i in range(1, ids_ref.shape[0]):
        member = jnp.logical_or(member, ids_ref[i : i + 1] == expert_i)
    row_i = lax.broadcasted_iota(jnp.int32, (seq, seq), 0)
    col_i = lax.broadcasted_iota(jnp.int32, (seq, seq), 1)

    if n_head > 1:
        drain(logit.at[pl.ds(0, n_head - 1)], lr)
    total = logit[0]
    for i in range(1, n_head):
        total = total + logit[i]
    total = jnp.where(member, total, -jnp.inf)
    top = jnp.max(total, axis=0, keepdims=True)
    weights = jnp.exp(total - top)
    weights = weights / jnp.sum(weights, axis=0, keepdims=True)
    weights_t = jnp.where(member, weights, -1.0)
    for c in range(cols):
        gt[c] = weights_t[c * pair : (c + 1) * pair]

    def gate_copy(c):
        return send(gt.at[c], gates.at[z], GATE, gr.at[z], exp_peer(c))

    def gate_wait(c):
        return send(gt.at[c], gates.at[c], GATE, gr.at[c], exp_peer(c))

    def far():
        if cols > 2:
            @pl.when(z == 0)
            def _():
                pl.semaphore_wait(down_sem, 1)

            @pl.when(z == cols - 1)
            def _():
                pl.semaphore_wait(up_sem, 1)

    if cols != 4:
        far()
    for i, c in enumerate(reversed(col_peers)):
        gate_copy(c).start()
        if cols == 4 and i == 0:
            far()

    earlier = (row_i < col_i).astype(BF16)
    slot_i = lax.broadcasted_iota(jnp.int32, (room, seq), 0)
    seq_i = lax.broadcasted_iota(jnp.int32, (n_exp, seq), 0)
    gg_copy.wait_recv()

    def contribution(c, w):
        named = w >= 0.0
        before = mm(jnp.where(named, 1.0, 0.0).astype(BF16), earlier).astype(jnp.int32)
        slot_grads = []
        spread = []
        for j in range(pair):
            hit = jnp.logical_and(before[j : j + 1] == slot_i, named[j : j + 1])
            spread.append(jnp.where(hit, w[j : j + 1], 0.0).astype(BF16))
            own_g = gg_ref[j % local].astype(F32)
            far_g = gg_in[j % local].astype(F32)
            table = jnp.where(x == j // local, own_g, far_g).astype(BF16)
            by_seq = mm(table, jnp.where(hit[:cap], 1.0, 0.0).astype(BF16))
            slot_grads.append(
                jnp.sum(jnp.where(seq_i == 2 * c + x, by_seq, 0.0), axis=0, keepdims=True)
            )
        return jnp.concatenate(spread, axis=0), slot_grads

    def weigh(c, spread):
        return mm(spread, rows[c].reshape(pair * room, width), TN)

    def row_wait(c):
        drain(rows.at[c, 1 - x], xr.at[c])

    def part_copy(c):
        return send(p_out.at[c], p_in.at[z], PART, pr.at[z], exp_peer(c))

    def slot_copy(c):
        return send(sg_out.at[c], sg_in.at[z], SLOT, sr, exp_peer(c))

    spread_z, slot_grads = contribution(z, gt[z])
    for j in range(pair):
        sg_in[z, j : j + 1] = slot_grads[j]
    for i, c in enumerate(col_peers):
        gate_wait(c).wait_recv()
        spread, slot_grads = contribution(c, gates[c])
        for j in range(pair):
            sg_out[c, j : j + 1] = slot_grads[j]
        slot_copy(c).start()
        row_wait(c)
        p_out[c] = weigh(c, spread).astype(BF16)
        part_copy(c).start()
    if cols > 1:
        drain(sg_in.at[pl.ds(0, cols - 1)], sr)
    mean = jnp.zeros((1, seq), F32)
    for c in range(cols):
        mean = mean + jnp.sum(jnp.maximum(gt[c], 0.0) * sg_in[c], axis=0, keepdims=True)
    for c in range(cols):
        diff_v[c * pair : (c + 1) * pair] = jnp.maximum(gt[c], 0.0) * (sg_in[c] - mean)
    diff = diff_v[...]
    diff_hi = diff.astype(BF16)
    diff_lo = (diff - diff_hi.astype(F32)).astype(BF16)
    grad = mm(diff_hi, router_ref[...], TN) + mm(diff_lo, router_ref[...], TN)
    loads["og"].wait()
    loads["scale"].wait()
    scale = jnp.sum(
        jnp.where(row_i == col_i, jnp.broadcast_to(scale_ref[...], (seq, seq)), 0.0),
        axis=1, keepdims=True,
    )
    row_wait(z)
    grad = grad + weigh(z, spread_z)
    for i, c in enumerate(col_peers):
        drain(p_in.at[c], pr.at[c])
        grad = grad + p_in[c].astype(F32)


    def gh_copy(src, k, to):
        return send(
            gh_all.at[src, k], gh_all.at[src, k], GH, hr.at[src, k], {"head": to}
        )

    def half_of(a, k):
        return a[:, k * half : (k + 1) * half]

    base = []
    for k in range(2):
        base.append(
            half_of(og_ref[...], k).astype(F32) + scale * (half_of(gain, k) * half_of(grad, k))
        )
        gh_all[h, k] = base[k].astype(BF16)
        for p in [sibling] + same:
            gh_copy(h, k, p).start()
    for p in cross:
        for k in range(2):
            gh_copy(h, k, p).start()
    inner_v[h] = jnp.broadcast_to(
        jnp.sum(hidden_f32() * gain * grad, axis=1, keepdims=True), (seq, HEAD_WIDTH)
    )

    def inner_copy(src, to):
        return send(inner_v.at[src], inner_v.at[src], INNER, inr, {"head": to})

    for p in head_peers:
        inner_copy(h, p).start()
    drain(w_v, w_sem)
    if n_head > 1:
        drain(x_all.at[pl.ds(0, n_head - 1)], xar)

    rows_w = w_v.shape[1]
    tile = min(512, rows_w)
    per = tile // HEAD_WIDTH

    def piece(p, k):
        return (
            jnp.concatenate([gh_all[p, k], x_all[p, :, k * half : (k + 1) * half]], axis=0),
            k * half, half,
        )

    def whole(p):
        return (
            jnp.concatenate(
                [jnp.concatenate([gh_all[p, 0], gh_all[p, 1]], axis=1), x_all[p]], axis=0
            ),
            0, width,
        )

    def product(p, block, r):
        a, at, size = block
        return mm(a, w_v[p, r : r + tile, at : at + size], NT)

    stages = [(h, None)] + [(sibling, None)]
    for p in same + cross:
        stages += [(p, 0), (p, 1)]
    for i, (p, k) in enumerate(stages[:-1]):
        if i:
            for kk in (0, 1) if k is None else (k,):
                drain(gh_all.at[p, kk], hr.at[p, kk])
        block = whole(p) if k is None else piece(p, k)
        for r in range(0, rows_w, tile):
            part = product(p, block, r)
            if i:
                part = ctx[:, r : r + tile] + part
            ctx[:, r : r + tile] = part

    if n_head > 1:
        drain(inner_v.at[pl.ds(0, n_head - 1)], inr)
    inner = inner_v[0]
    for i in range(1, n_head):
        inner = inner + inner_v[i]
    taken = scale * inner[:, 0:1] / width_total

    p, k = stages[-1]
    if k is None:
        for kk in (0, 1):
            drain(gh_all.at[p, kk], hr.at[p, kk])
        block = whole(p)
    else:
        drain(gh_all.at[p, k], hr.at[p, k])
        block = piece(p, k)
    key_block = k_ref[:, lanes]
    value_block = v_ref[:, lanes]
    gk = jnp.zeros((seq, HEAD_WIDTH), F32)
    gv = jnp.zeros((seq, HEAD_WIDTH), F32)

    def q_copy(r, to):
        at = pl.ds(r, tile)
        return send(q_send.at[to, :, at], q_in.at[h, :, at], QS, qr, {"head": to})

    def kv_copy(to):
        return send(kv_send.at[to], kv_in.at[h], KVS, kvr, {"head": to})

    for r in range(0, rows_w, tile):
        part = ctx[:, r : r + tile] + product(p, block, r)
        ctx_s = stacked((part[:seq] - taken * part[seq:]).astype(BF16))
        first = r // HEAD_WIDTH
        probs = probs_v[first * seq : (first + per) * seq]
        prob_grads = mm(ctx_s, value_block, NT)
        delta = jnp.sum(probs * prob_grads, axis=1, keepdims=True)
        score_grads = (probs * (prob_grads - delta) * inv_sqrt).astype(BF16)
        gq = mm(score_grads, key_block).astype(BF16)
        for d in range(n_head):
            for i in range(per):
                s = i * seq + d * tok
                q_send[d, :, r + i * HEAD_WIDTH : r + (i + 1) * HEAD_WIDTH] = gq[s : s + tok]
        for to in head_peers:
            q_copy(r, to).start()
        gk = gk + mm(score_grads, stacked(q_ref[:, r : r + tile]), TN)
        gv = gv + mm(probs.astype(BF16), ctx_s, TN)
    for d in range(n_head):
        kv_send[d, 0] = gk[d * tok : (d + 1) * tok].astype(BF16)
        kv_send[d, 1] = gv[d * tok : (d + 1) * tok].astype(BF16)
    for to in head_peers:
        kv_copy(to).start()
    for k in range(2):
        gh_out[:, k * half : (k + 1) * half] = (
            base[k] - half_of(hidden_f32(), k) * taken
        ).astype(BF16)
    q_in[h] = q_send[h]
    kv_in[h] = kv_send[h]

    others = pl.ds(0, n_head - 1)
    some_cols = pl.ds(0, cols - 1)
    sent = [(row_send, ROWS)]
    if cols > 1:
        sent += [(gt.at[some_cols], GATE), (p_out.at[some_cols], PART), (sg_out.at[some_cols], SLOT)]
    if n_head > 1:
        sent += [
            (logit.at[others], LOGIT), (x_all.at[others], XALL), (gh_all.at[others], GH),
            (inner_v.at[others], INNER),
        ]
    gg_copy.wait_send()
    for ref, which in sent:
        drain(ref, send_sem.at[which])
    if n_head > 1:
        drain(q_in.at[others], qr)
        drain(kv_in.at[others], kvr)
    span = heads * HEAD_WIDTH
    for i in range(n_head):
        gq_out[:, i * span : (i + 1) * span] = q_in[i]
    replicas = n_head // KEY_VALUE_HEADS
    for g in range(KEY_VALUE_HEADS):
        for k, out in enumerate((gk_out, gv_out)):
            total = kv_in[g * replicas, k].astype(F32)
            for i in range(1, replicas):
                total = total + kv_in[g * replicas + i, k].astype(F32)
            out[:, g * HEAD_WIDTH : (g + 1) * HEAD_WIDTH] = total.astype(BF16)
    if n_head > 1:
        drain(q_send.at[others], send_sem.at[QS])
        drain(kv_send.at[others], send_sem.at[KVS])


def write_out(*refs):
    n = (len(refs) - 1) // 2
    sems = refs[-1]
    copies = [
        pltpu.make_async_copy(refs[i], refs[n + i], sems.at[i]) for i in range(n)
    ]
    for cp in copies:
        cp.start()
    for cp in copies:
        cp.wait()


def solution(mesh):
    n_exp = mesh.shape["exp"]
    n_head = mesh.shape["head"]
    cols = n_exp // 2

    def per_device(
        normed_input, norm_gain, norm_scale, out_grad, router_weight, routed_experts,
        expert_grad, gate_grad, out_proj, query_states, rotated_keys, value_tensor,
    ):
        _, seq, width = normed_input.shape
        experts_all = router_weight.shape[1]
        local, _, cap, _ = expert_grad.shape
        pair = 2 * local
        span, width_total = out_proj.shape
        heads = span // HEAD_WIDTH
        tok = seq // n_head
        kv_width = rotated_keys.shape[2]
        vm = pltpu.VMEM
        dma = pltpu.SemaphoreType.DMA
        vmem = pl.BlockSpec(memory_space=pltpu.VMEM)
        hbm = pl.BlockSpec(memory_space=pltpu.HBM)
        room = -(-cap // 16) * 16
        top_k = routed_experts.shape[2]
        outs = pl.pallas_call(
            functools.partial(kernel, n_exp, n_head, width_total),
            name="moe_attention_backward",
            out_shape=(
                jax.ShapeDtypeStruct((seq, width), BF16),
                jax.ShapeDtypeStruct((tok, n_head * span), BF16),
                jax.ShapeDtypeStruct((tok, kv_width), BF16),
                jax.ShapeDtypeStruct((tok, kv_width), BF16),
            ),
            in_specs=[hbm] * 12,
            out_specs=(vmem,) * 4,
            scratch_shapes=[
                vm((1, width), F32), vm((1, seq), F32),
                vm((seq, width), BF16), vm((experts_all, width), BF16),
                vm((top_k, seq), jnp.int32), vm((local, cap, n_exp, width), BF16),
                vm(gate_grad.shape, BF16), vm((seq, span), BF16),
                vm((seq, kv_width), BF16), vm((seq, kv_width), BF16), dma((11,)),
                vm((n_head, span, width), BF16),
                vm((cols, local * room, width), BF16),
                vm((cols, 2, local * room, width), BF16),
                vm(gate_grad.shape, BF16),
                vm((n_head, experts_all, seq), F32),
                vm((cols, pair, seq), F32),
                vm((cols, pair, seq), F32),
                vm((cols, seq, width), BF16),
                vm((cols, seq, width), BF16),
                vm((cols, pair, seq), F32),
                vm((cols, pair, seq), F32),
                vm((experts_all, seq), F32),
                vm((n_head, seq, HEAD_WIDTH), F32),
                vm((n_head, 2, seq, width // 2), BF16),
                vm((n_head, seq, width), BF16),
                vm((2 * seq, span), F32),
                vm((heads * seq, seq), F32),
                vm((n_head, tok, span), BF16),
                vm((n_head, tok, span), BF16),
                vm((n_head, 2, tok, HEAD_WIDTH), BF16),
                vm((n_head, 2, tok, HEAD_WIDTH), BF16),
                dma, dma((11,)), dma((cols,)), dma, dma, dma((cols,)), dma((cols,)), dma,
                dma, dma((n_head, 2)), dma, dma, dma,
                pltpu.SemaphoreType.REGULAR, pltpu.SemaphoreType.REGULAR,
            ],
            compiler_params=pltpu.CompilerParams(
                collective_id=0, has_side_effects=True, vmem_limit_bytes=48 * 1024 * 1024
            ),
        )(
            *(
                pltpu.with_memory_space_constraint(a, pltpu.HBM)
                for a in (
                    normed_input[0], norm_gain[None], norm_scale, out_grad[0], router_weight.T,
                    routed_experts[0].T, jnp.transpose(expert_grad, (0, 2, 1, 3)), gate_grad,
                    out_proj, query_states[0], rotated_keys[0], value_tensor[0],
                )
            )
        )
        outs = pl.pallas_call(
            write_out,
            name="write_out",
            out_shape=tuple(jax.ShapeDtypeStruct(o.shape, o.dtype) for o in outs),
            in_specs=[vmem] * 4,
            out_specs=(hbm,) * 4,
            scratch_shapes=[dma((4,))],
            compiler_params=pltpu.CompilerParams(vmem_limit_bytes=1024 * 1024),
        )(*outs)
        return tuple(o[None] for o in outs)

    placed = (
        P("exp", None, "head"),
        P("head"),
        P("exp", None),
        P("exp", None, "head"),
        P("head", None),
        P("exp", None, None),
        P("exp", None, None, "head"),
        P("exp", None, None),
        P("head", None),
        P("exp", None, "head"),
        P("exp", None, None),
        P("exp", None, None),
    )
    return jax.shard_map(
        per_device,
        mesh=mesh,
        in_specs=placed,
        out_specs=(
            P("exp", None, "head"),
            P("exp", "head", None),
            P("exp", "head", None),
            P("exp", "head", None),
        ),
        check_vma=False,
    )
```

time: 32.2 us -> 31.3 us (0.972)
  Pallas kernels: 31.4 us -> 30.5 us
    pallas_call x1, Pallas kernels: 30.7 us -> 29.8 us  [per_device(): pl.pallas_call(functools.partial(kernel, n_exp, n_head, width_total), nam...]
where the time goes in v1:
time: 31.3 us; the launch traced here: 31.1 us
  Pallas kernels  30.5 us (97%)
  between operations  0.64 us (2%)
    pallas_call x1, Pallas kernels, per_device(): pl.pallas_call(functools.partial(kernel, n_exp, n_head, width_total), nam...  29.8 us
    pallas_call x1, Pallas kernels, per_device(): pl.pallas_call(write_out, name='write_out', out_shape=tuple((jax.ShapeDty...  0.72 us

profile of v1, /device:TPU:0, one launch (start us, length us, event | category | flops | bytes accessed | tf_op | source)
XLA Modules:
  0.0 31.1 jit_solution(13891948309013328694)
XLA Ops:
  0.6 29.8 %moe_attention_backward.1 = (bf16[32,1024]{1,0:T(8,128)(2,1)S(1)}, bf16[8,8192]{1,0:T(8,128)(2,1)S(1)}, bf16[8,512]{1,0:T(8,128)(2,1)S(1)}, bf16[8,512]{1,0:T(8,128)(2,1)S(1)}) custom-call(bf16[32,1024]{1,0:T(8,128)(2,1)} %bitcast.17, f32[1,1024]{1,0:T(1,128)} %bitcast.22, f32[1,32]{1,0:T(1,128)} %scale_hbm.1, bf16[32,1024]{1,0:T(8,128)(2,1)} %bitcast.18, ...), custom_call_target="tpu_custom_call" | custom-call | tf_op jit(solution)/shard_map/moe_attention_backward/pallas_call | solution.py:518
  30.4 0.7 %write_out.1 = (bf16[32,1024]{1,0:T(8,128)(2,1)}, bf16[8,8192]{1,0:T(8,128)(2,1)}, bf16[8,512]{1,0:T(8,128)(2,1)}, bf16[8,512]{1,0:T(8,128)(2,1)}) custom-call(bf16[32,1024]{1,0:T(8,128)(2,1)S(1)} %get-tuple-element.12.refs_0_, bf16[8,8192]{1,0:T(8,128)(2,1)S(1)} %get-tuple-element.13.refs_1_, bf16[8,512]{1,0:T(8,128)(2,1)S(1)} %get-tuple-element.14.refs_2_, ...), custom_call_target="tpu_custom_call" | custom-call | tf_op jit(solution)/shard_map/write_out/pallas_call | solution.py:573

commit v2 on v1

--- a/solution.py
+++ b/solution.py
@@ -30,8 +30,8 @@
     gain_ref, scale_ref, og_ref, router_ref, ids_ref, expert_ref, gg_ref,
     q_ref, k_ref, v_ref, in_sem,
     w_v, row_send, rows, gg_in, logit, gt, gates, p_out, p_in, sg_out, sg_in, diff_v, inner_v, gh_all, x_all,
-    ctx, probs_v, q_send, q_in, kv_send, kv_in,
-    w_sem, send_sem, xr, ggr, lr, gr, pr, sr, inr, hr, xar, qr, kvr, up_sem, down_sem,
+    ctx, probs_v, q_send, q_in, kv_send, kv_in, across, across_out, s_out, s_in,
+    w_sem, send_sem, xr, ggr, lr, gr, pr, sr, inr, hr, xar, qr, kvr, acr, shr, up_sem, down_sem,
 ):
     e = lax.axis_index("exp")
     h = lax.axis_index("head")
@@ -47,7 +47,7 @@
     tok = seq // n_head
     half = width // 2
     partner = 2 * z + 1 - x
-    ROWS, GG, LOGIT, GATE, PART, SLOT, GH, INNER, XALL, QS, KVS = range(11)
+    ROWS, GG, LOGIT, GATE, PART, SLOT, GH, INNER, XALL, QS, KVS, ACROSS, SHARE = range(13)
 
     def exp_peer(i):
         return {"exp": 2 * i + x}
@@ -70,10 +70,7 @@
         same.append(there + core)
         cross.append(there + 1 - core)
     head_peers = [sibling] + same + cross
-    if cols == 4:
-        col_peers = [3 * (1 - z // 2), 2 - z // 2, z + 1 - 2 * lax.rem(z, 2)]
-    else:
-        col_peers = [lax.rem(z + i, cols) for i in range(1, cols)]
+    col_peers = [i + (i + cols - z) // cols for i in range(cols - 1)]
     all_cols = col_peers + [z]
 
     barrier = pltpu.get_barrier_semaphore()
@@ -159,8 +156,10 @@
 
     def row_copy(c, j):
         part = pl.ds(j * room, room)
-        return send(row_send.at[c, part], rows.at[c, x, part], ROWS, xr.at[c], {"exp": partner})
-
+        return send(row_send.at[c, part], rows.at[c, 1, part], ROWS, xr.at[c], {"exp": partner})
+
+    row_order = [(c, j) for c in col_peers for j in range(local)]
+    held = len(row_order) // 2
     step = min(cols, 4)
     for first in range(0, cols, step):
         some = all_cols[first : first + step]
@@ -169,10 +168,10 @@
             got = mm(chosen, flat[j]).astype(BF16)
             for i, c in enumerate(some):
                 row_send[c, j * room : (j + 1) * room] = got[i * room : (i + 1) * room]
-            row_copy(some[0], j).start()
-        for c in some[1:]:
-            for j in range(local):
-                row_copy(c, j).start()
+            if cols > 1 and not first:
+                row_copy(*row_order[j]).start()
+    for c, j in row_order[local:held]:
+        row_copy(c, j).start()
 
     for first in range(0, cols, step):
         some = all_cols[first : first + step]
@@ -180,7 +179,7 @@
         for j in range(local):
             got = mm(chosen, flat[j]).astype(BF16)
             for i, c in enumerate(some):
-                rows[c, x, j * room : (j + 1) * room] = got[i * room : (i + 1) * room]
+                rows[c, 0, j * room : (j + 1) * room] = got[i * room : (i + 1) * room]
 
     if cols > 3:
         @pl.when(jnp.logical_and(z > 1, z < cols - 1))
@@ -238,6 +237,10 @@
     def gate_wait(c):
         return send(gt.at[c], gates.at[c], GATE, gr.at[c], exp_peer(c))
 
+    def by_side(a):
+        low, high = a[:local], a[local:]
+        return jnp.where(x == 0, low, high), jnp.where(x == 0, high, low)
+
     def far():
         if cols > 2:
             @pl.when(z == 0)
@@ -248,40 +251,53 @@
             def _():
                 pl.semaphore_wait(up_sem, 1)
 
-    if cols != 4:
-        far()
-    for i, c in enumerate(reversed(col_peers)):
+    across_out[...] = by_side(gt[z])[1]
+    across_copy = send(across_out, across, ACROSS, acr, {"exp": partner})
+    across_copy.start()
+    for c, j in row_order[held:]:
+        row_copy(c, j).start()
+    far()
+    for c in col_peers:
         gate_copy(c).start()
-        if cols == 4 and i == 0:
-            far()
 
     earlier = (row_i < col_i).astype(BF16)
     slot_i = lax.broadcasted_iota(jnp.int32, (room, seq), 0)
     seq_i = lax.broadcasted_iota(jnp.int32, (n_exp, seq), 0)
     gg_copy.wait_recv()
 
-    def contribution(c, w):
+    def places(w):
         named = w >= 0.0
         before = mm(jnp.where(named, 1.0, 0.0).astype(BF16), earlier).astype(jnp.int32)
-        slot_grads = []
-        spread = []
+        hits = []
+        for j in range(w.shape[0]):
+            hits.append(jnp.logical_and(before[j : j + 1] == slot_i, named[j : j + 1]))
+        spread = [jnp.where(hit, w[j : j + 1], 0.0).astype(BF16) for j, hit in enumerate(hits)]
+        return spread, hits
+
+    def contribution(c, w, into):
+        spread, hits = places(jnp.concatenate(by_side(w), axis=0))
+        slots = []
         for j in range(pair):
-            hit = jnp.logical_and(before[j : j + 1] == slot_i, named[j : j + 1])
-            spread.append(jnp.where(hit, w[j : j + 1], 0.0).astype(BF16))
-            own_g = gg_ref[j % local].astype(F32)
-            far_g = gg_in[j % local].astype(F32)
-            table = jnp.where(x == j // local, own_g, far_g).astype(BF16)
-            by_seq = mm(table, jnp.where(hit[:cap], 1.0, 0.0).astype(BF16))
-            slot_grads.append(
+            table = (gg_ref if j < local else gg_in)[j % local]
+            by_seq = mm(table, jnp.where(hits[j][:cap], 1.0, 0.0).astype(BF16))
+            slots.append(
                 jnp.sum(jnp.where(seq_i == 2 * c + x, by_seq, 0.0), axis=0, keepdims=True)
             )
-        return jnp.concatenate(spread, axis=0), slot_grads
-
-    def weigh(c, spread):
-        return mm(spread, rows[c].reshape(pair * room, width), TN)
+        for j in range(pair):
+            into[c, j : j + 1] = jnp.where(x == 0, slots[j], slots[(j + local) % pair])
+        return jnp.concatenate(spread, axis=0)
 
     def row_wait(c):
-        drain(rows.at[c, 1 - x], xr.at[c])
+        drain(rows.at[c, 1], xr.at[c])
+
+    s_copy = send(s_out, s_in, SHARE, shr, {"exp": partner})
+
+    def share():
+        across_copy.wait_recv()
+        s_out[...] = mm(
+            jnp.concatenate(places(across[...])[0], axis=0), row_send[z], TN
+        ).astype(BF16)
+        s_copy.start()
 
     def part_copy(c):
         return send(p_out.at[c], p_in.at[z], PART, pr.at[z], exp_peer(c))
@@ -289,18 +305,19 @@
     def slot_copy(c):
         return send(sg_out.at[c], sg_in.at[z], SLOT, sr, exp_peer(c))
 
-    spread_z, slot_grads = contribution(z, gt[z])
-    for j in range(pair):
-        sg_in[z, j : j + 1] = slot_grads[j]
+    spread_z = contribution(z, gt[z], sg_in)
+    grad = mm(spread_z[: local * room], rows[z, 0], TN)
     for i, c in enumerate(col_peers):
         gate_wait(c).wait_recv()
-        spread, slot_grads = contribution(c, gates[c])
-        for j in range(pair):
-            sg_out[c, j : j + 1] = slot_grads[j]
+        spread = contribution(c, gates[c], sg_out)
         slot_copy(c).start()
         row_wait(c)
-        p_out[c] = weigh(c, spread).astype(BF16)
+        p_out[c] = mm(spread, rows[c].reshape(pair * room, width), TN).astype(BF16)
         part_copy(c).start()
+        if i == 0:
+            share()
+    if cols == 1:
+        share()
     if cols > 1:
         drain(sg_in.at[pl.ds(0, cols - 1)], sr)
     mean = jnp.zeros((1, seq), F32)
@@ -311,15 +328,15 @@
     diff = diff_v[...]
     diff_hi = diff.astype(BF16)
     diff_lo = (diff - diff_hi.astype(F32)).astype(BF16)
-    grad = mm(diff_hi, router_ref[...], TN) + mm(diff_lo, router_ref[...], TN)
+    grad = grad + mm(diff_hi, router_ref[...], TN) + mm(diff_lo, router_ref[...], TN)
     loads["og"].wait()
     loads["scale"].wait()
     scale = jnp.sum(
         jnp.where(row_i == col_i, jnp.broadcast_to(scale_ref[...], (seq, seq)), 0.0),
         axis=1, keepdims=True,
     )
-    row_wait(z)
-    grad = grad + weigh(z, spread_z)
+    s_copy.wait_recv()
+    grad = grad + s_in[...].astype(F32)
     for i, c in enumerate(col_peers):
         drain(p_in.at[c], pr.at[c])
         grad = grad + p_in[c].astype(F32)
@@ -359,7 +376,8 @@
 
     rows_w = w_v.shape[1]
     tile = min(512, rows_w)
-    per = tile // HEAD_WIDTH
+    group = max(rows_w // 2, HEAD_WIDTH)
+    per = group // HEAD_WIDTH
 
     def piece(p, k):
         return (
@@ -414,14 +432,16 @@
     gv = jnp.zeros((seq, HEAD_WIDTH), F32)
 
     def q_copy(r, to):
-        at = pl.ds(r, tile)
+        at = pl.ds(r, group)
         return send(q_send.at[to, :, at], q_in.at[h, :, at], QS, qr, {"head": to})
 
     def kv_copy(to):
         return send(kv_send.at[to], kv_in.at[h], KVS, kvr, {"head": to})
 
     for r in range(0, rows_w, tile):
-        part = ctx[:, r : r + tile] + product(p, block, r)
+        ctx[:, r : r + tile] = ctx[:, r : r + tile] + product(p, block, r)
+    for r in range(0, rows_w, group):
+        part = ctx[:, r : r + group]
         ctx_s = stacked((part[:seq] - taken * part[seq:]).astype(BF16))
         first = r // HEAD_WIDTH
         probs = probs_v[first * seq : (first + per) * seq]
@@ -435,7 +455,7 @@
                 q_send[d, :, r + i * HEAD_WIDTH : r + (i + 1) * HEAD_WIDTH] = gq[s : s + tok]
         for to in head_peers:
             q_copy(r, to).start()
-        gk = gk + mm(score_grads, stacked(q_ref[:, r : r + tile]), TN)
+        gk = gk + mm(score_grads, stacked(q_ref[:, r : r + group]), TN)
         gv = gv + mm(probs.astype(BF16), ctx_s, TN)
     for d in range(n_head):
         kv_send[d, 0] = gk[d * tok : (d + 1) * tok].astype(BF16)
@@ -451,15 +471,19 @@
 
     others = pl.ds(0, n_head - 1)
     some_cols = pl.ds(0, cols - 1)
-    sent = [(row_send, ROWS)]
+    sent = []
     if cols > 1:
-        sent += [(gt.at[some_cols], GATE), (p_out.at[some_cols], PART), (sg_out.at[some_cols], SLOT)]
+        sent += [
+            (row_send.at[some_cols], ROWS),
+            (gt.at[some_cols], GATE), (p_out.at[some_cols], PART), (sg_out.at[some_cols], SLOT)]
     if n_head > 1:
         sent += [
             (logit.at[others], LOGIT), (x_all.at[others], XALL), (gh_all.at[others], GH),
             (inner_v.at[others], INNER),
         ]
     gg_copy.wait_send()
+    across_copy.wait_send()
+    s_copy.wait_send()
     for ref, which in sent:
         drain(ref, send_sem.at[which])
     if n_head > 1:
@@ -553,8 +577,10 @@
                 vm((n_head, tok, span), BF16),
                 vm((n_head, 2, tok, HEAD_WIDTH), BF16),
                 vm((n_head, 2, tok, HEAD_WIDTH), BF16),
-                dma, dma((11,)), dma((cols,)), dma, dma, dma((cols,)), dma((cols,)), dma,
-                dma, dma((n_head, 2)), dma, dma, dma,
+                vm((local, seq), F32), vm((local, seq), F32),
+                vm((seq, width), BF16), vm((seq, width), BF16),
+                dma, dma((13,)), dma((cols,)), dma, dma, dma((cols,)), dma((cols,)), dma,
+                dma, dma((n_head, 2)), dma, dma, dma, dma, dma,
                 pltpu.SemaphoreType.REGULAR, pltpu.SemaphoreType.REGULAR,
             ],
             compiler_params=pltpu.CompilerParams(

time: 31.3 us -> 29.7 us (0.949)
  the two profiles are of different devices: /device:TPU:0 before, /device:TPU:25 now
where the time goes in v2:
time: 29.7 us; the launch traced here: 29.5 us
  Pallas kernels  28.9 us (97%)
  between operations  0.64 us (2%)
    pallas_call x1, Pallas kernels, per_device(): pl.pallas_call(functools.partial(kernel, n_exp, n_head, width_total), nam...  28.2 us
    pallas_call x1, Pallas kernels, per_device(): pl.pallas_call(write_out, name='write_out', out_shape=tuple((jax.ShapeDty...  0.72 us

profile of v2, /device:TPU:25, one launch (start us, length us, event | category | flops | bytes accessed | tf_op | source)
XLA Modules:
  0.0 29.5 jit_solution(14967013304123083422)
XLA Ops:
  0.6 28.2 %moe_attention_backward.1 = (bf16[32,1024]{1,0:T(8,128)(2,1)S(1)}, bf16[8,8192]{1,0:T(8,128)(2,1)S(1)}, bf16[8,512]{1,0:T(8,128)(2,1)S(1)}, bf16[8,512]{1,0:T(8,128)(2,1)S(1)}) custom-call(bf16[32,1024]{1,0:T(8,128)(2,1)} %bitcast.17, f32[1,1024]{1,0:T(1,128)} %bitcast.22, f32[1,32]{1,0:T(1,128)} %scale_hbm.1, bf16[32,1024]{1,0:T(8,128)(2,1)} %bitcast.18, ...), custom_call_target="tpu_custom_call" | custom-call | tf_op jit(solution)/shard_map/moe_attention_backward/pallas_call | solution.py:542
  28.8 0.7 %write_out.1 = (bf16[32,1024]{1,0:T(8,128)(2,1)}, bf16[8,8192]{1,0:T(8,128)(2,1)}, bf16[8,512]{1,0:T(8,128)(2,1)}, bf16[8,512]{1,0:T(8,128)(2,1)}) custom-call(bf16[32,1024]{1,0:T(8,128)(2,1)S(1)} %get-tuple-element.12.refs_0_, bf16[8,8192]{1,0:T(8,128)(2,1)S(1)} %get-tuple-element.13.refs_1_, bf16[8,512]{1,0:T(8,128)(2,1)S(1)} %get-tuple-element.14.refs_2_, ...), custom_call_target="tpu_custom_call" | custom-call | tf_op jit(solution)/shard_map/write_out/pallas_call | solution.py:599

commit v3 on v2

--- a/solution.py
+++ b/solution.py
@@ -30,8 +30,8 @@
     gain_ref, scale_ref, og_ref, router_ref, ids_ref, expert_ref, gg_ref,
     q_ref, k_ref, v_ref, in_sem,
     w_v, row_send, rows, gg_in, logit, gt, gates, p_out, p_in, sg_out, sg_in, diff_v, inner_v, gh_all, x_all,
-    ctx, probs_v, q_send, q_in, kv_send, kv_in, across, across_out, s_out, s_in,
-    w_sem, send_sem, xr, ggr, lr, gr, pr, sr, inr, hr, xar, qr, kvr, acr, shr, up_sem, down_sem,
+    ctx, probs_v, q_send, q_in, kv_send, kv_in, across, across_out, s_out, s_in, diag_in, diag_out, far_out, far_in, spread_v, grad_v,
+    w_sem, send_sem, xr, ggr, lr, gr, pr, sr, inr, hr, xar, qr, kvr, acr, shr, dgr, fr, up_sem, down_sem, side_sem,
 ):
     e = lax.axis_index("exp")
     h = lax.axis_index("head")
@@ -47,7 +47,7 @@
     tok = seq // n_head
     half = width // 2
     partner = 2 * z + 1 - x
-    ROWS, GG, LOGIT, GATE, PART, SLOT, GH, INNER, XALL, QS, KVS, ACROSS, SHARE = range(13)
+    ROWS, GG, LOGIT, GATE, PART, SLOT, GH, INNER, XALL, QS, KVS, ACROSS, SHARE, FAR, DIAG = range(15)
 
     def exp_peer(i):
         return {"exp": 2 * i + x}
@@ -70,8 +70,16 @@
         same.append(there + core)
         cross.append(there + 1 - core)
     head_peers = [sibling] + same + cross
-    col_peers = [i + (i + cols - z) // cols for i in range(cols - 1)]
-    all_cols = col_peers + [z]
+    paired = cols > 1
+    if paired:
+        edge = z // (cols - 1)
+        near = z + 1 - 2 * edge
+        row_cols = [i + 2 * ((i + cols - z + edge) // cols) for i in range(cols - 2)]
+        col_peers = [near] + row_cols
+    else:
+        row_cols = []
+        col_peers = []
+    all_cols = row_cols + ([near] if paired else []) + [z]
 
     barrier = pltpu.get_barrier_semaphore()
     pl.semaphore_signal(barrier, inc=1, device_id={"exp": partner}, device_id_type=MESH)
@@ -90,8 +98,8 @@
 
     loads = {}
     for i, (name, src, dst) in enumerate((
-        ("x", x_hbm, x_all.at[h]), ("gain", gain_hbm, gain_ref), ("router", router_hbm, router_ref),
-        ("expert", expert_hbm, expert_ref), ("gg", gg_hbm, gg_ref), ("ids", ids_hbm, ids_ref),
+        ("expert", expert_hbm, expert_ref), ("x", x_hbm, x_all.at[h]), ("gain", gain_hbm, gain_ref),
+        ("router", router_hbm, router_ref), ("gg", gg_hbm, gg_ref), ("ids", ids_hbm, ids_ref),
         ("q", q_hbm, q_ref), ("k", k_hbm, k_ref), ("v", v_hbm, v_ref), ("og", og_hbm, og_ref),
         ("scale", scale_hbm, scale_ref),
     )):
@@ -103,43 +111,7 @@
         for j in range(n_head)
     ]
 
-    for name in ("x", "gain", "router"):
-        loads[name].wait()
-    gain = gain_ref[...]
-
-    def hidden_f32():
-        return x_all[h].astype(F32)
-
-    logit[h] = mm(router_ref[...], (hidden_f32() * gain).astype(BF16), NT)
-    pl.semaphore_wait(barrier, greeted)
-
-    def logit_copy(src, to):
-        return send(logit.at[src], logit.at[src], LOGIT, lr, {"head": to})
-
-    def x_copy(src, to):
-        return send(x_all.at[src], x_all.at[src], XALL, xar, {"head": to})
-
-    for p in head_peers:
-        logit_copy(h, p).start()
-
-    if cols > 2:
-        @pl.when(z == 1)
-        def _():
-            pl.semaphore_signal(up_sem, inc=1, device_id=exp_peer(z + 1), device_id_type=MESH)
-
-        @pl.when(z == cols - 2)
-        def _():
-            pl.semaphore_signal(down_sem, inc=1, device_id=exp_peer(z - 1), device_id_type=MESH)
-
-    for p in head_peers:
-        x_copy(h, p).start()
-    loads["gg"].wait()
-    gg_copy = send(gg_ref, gg_in, GG, ggr, {"exp": partner})
-    gg_copy.start()
-
     loads["expert"].wait()
-    for cp in w_copies:
-        cp.start()
     flat = expert_ref.reshape(local, cap * n_exp, width)
 
     def pick(c_list, side):
@@ -158,29 +130,63 @@
         part = pl.ds(j * room, room)
         return send(row_send.at[c, part], rows.at[c, 1, part], ROWS, xr.at[c], {"exp": partner})
 
-    row_order = [(c, j) for c in col_peers for j in range(local)]
-    held = len(row_order) // 2
+    row_order = [(c, j) for c in row_cols for j in range(local)]
+    held = len(row_order) - len(row_order) // 4
     step = min(cols, 4)
-    for first in range(0, cols, step):
-        some = all_cols[first : first + step]
-        chosen = pick(some, 1 - x)
-        for j in range(local):
-            got = mm(chosen, flat[j]).astype(BF16)
-            for i, c in enumerate(some):
-                row_send[c, j * room : (j + 1) * room] = got[i * room : (i + 1) * room]
-            if cols > 1 and not first:
-                row_copy(*row_order[j]).start()
-    for c, j in row_order[local:held]:
+
+    def pick_all(side, into):
+        for first in range(0, cols, step):
+            some = all_cols[first : first + step]
+            chosen = pick(some, side)
+            for j in range(local):
+                got = mm(chosen, flat[j]).astype(BF16)
+                for i, c in enumerate(some):
+                    into(c)[j * room : (j + 1) * room] = got[i * room : (i + 1) * room]
+
+    pick_all(1 - x, lambda c: row_send.at[c])
+    loads["gg"].wait()
+    pl.semaphore_wait(barrier, greeted)
+    gg_copy = send(gg_ref, gg_in, GG, ggr, {"exp": partner})
+    gg_copy.start()
+    for c, j in row_order[:held]:
         row_copy(c, j).start()
-
-    for first in range(0, cols, step):
-        some = all_cols[first : first + step]
-        chosen = pick(some, x)
-        for j in range(local):
-            got = mm(chosen, flat[j]).astype(BF16)
-            for i, c in enumerate(some):
-                rows[c, 0, j * room : (j + 1) * room] = got[i * room : (i + 1) * room]
-
+    if paired:
+        pl.semaphore_signal(side_sem, inc=1, device_id={"exp": partner}, device_id_type=MESH)
+    if cols > 2:
+        @pl.when(z == 1)
+        def _():
+            pl.semaphore_signal(up_sem, inc=1, device_id=exp_peer(z + 1), device_id_type=MESH)
+
+        @pl.when(z == cols - 2)
+        def _():
+            pl.semaphore_signal(down_sem, inc=1, device_id=exp_peer(z - 1), device_id_type=MESH)
+
+    for name in ("x", "gain", "router"):
+        loads[name].wait()
+    gain = gain_ref[...]
+
+    def hidden_f32():
+        return x_all[h].astype(F32)
+
+    logit[h] = mm(router_ref[...], (hidden_f32() * gain).astype(BF16), NT)
+
+    def logit_copy(src, to):
+        return send(logit.at[src], logit.at[src], LOGIT, lr, {"head": to})
+
+    def x_copy(src, to):
+        return send(x_all.at[src], x_all.at[src], XALL, xar, {"head": to})
+
+    for p in head_peers:
+        logit_copy(h, p).start()
+    for p in head_peers:
+        x_copy(h, p).start()
+    for cp in w_copies:
+        cp.start()
+
+    pick_all(x, lambda c: rows.at[c, 0])
+
+    if paired:
+        pl.semaphore_wait(side_sem, 1)
     if cols > 3:
         @pl.when(jnp.logical_and(z > 1, z < cols - 1))
         def _():
@@ -251,13 +257,31 @@
             def _():
                 pl.semaphore_wait(up_sem, 1)
 
+    askers = [(z > 0, z - 1), (z == cols - 2, z + 1)]
+
+    def across_of(c):
+        return {"exp": 2 * c + 1 - x}
+
+    def diag_copy(k, to):
+        return send(diag_out.at[k], diag_in, DIAG + k, dgr, across_of(to))
+
+    def far_copy(k, to):
+        return send(far_out, far_in.at[k], FAR, fr.at[k], across_of(to))
+
     across_out[...] = by_side(gt[z])[1]
     across_copy = send(across_out, across, ACROSS, acr, {"exp": partner})
     across_copy.start()
+    if paired:
+        for k, (on, to) in enumerate(askers):
+            @pl.when(on)
+            def _():
+                diag_out[k] = by_side(gt[to])[1]
+                diag_copy(k, to).start()
+        gate_copy(near).start()
     for c, j in row_order[held:]:
         row_copy(c, j).start()
     far()
-    for c in col_peers:
+    for c in row_cols:
         gate_copy(c).start()
 
     earlier = (row_i < col_i).astype(BF16)
@@ -293,10 +317,12 @@
     s_copy = send(s_out, s_in, SHARE, shr, {"exp": partner})
 
     def share():
+        if paired:
+            diag_copy(0, near).wait_recv()
+            far_out[...] = shared(diag_in[...], near)
+            far_copy(edge, near).start()
         across_copy.wait_recv()
-        s_out[...] = mm(
-            jnp.concatenate(places(across[...])[0], axis=0), row_send[z], TN
-        ).astype(BF16)
+        s_out[...] = shared(across[...], z)
         s_copy.start()
 
     def part_copy(c):
@@ -307,17 +333,47 @@
 
     spread_z = contribution(z, gt[z], sg_in)
     grad = mm(spread_z[: local * room], rows[z, 0], TN)
-    for i, c in enumerate(col_peers):
+    def slots_to(c, k):
         gate_wait(c).wait_recv()
-        spread = contribution(c, gates[c], sg_out)
+        spread_v[k] = contribution(c, gates[c], sg_out)
         slot_copy(c).start()
+
+    def shared(w, c):
+        return mm(jnp.concatenate(places(w)[0], axis=0), row_send[c], TN).astype(BF16)
+
+    def whole_part(c, k):
         row_wait(c)
-        p_out[c] = mm(spread, rows[c].reshape(pair * room, width), TN).astype(BF16)
+        p_out[c] = mm(spread_v[k], rows[c].reshape(pair * room, width), TN).astype(BF16)
         part_copy(c).start()
-        if i == 0:
-            share()
-    if cols == 1:
-        share()
+
+    last = len(row_cols)
+
+    def near_part():
+        slots_to(near, last)
+        p_out[near] = mm(spread_v[last][: local * room], rows[near, 0], TN).astype(BF16)
+        part_copy(near).start()
+
+    def later_slots():
+        for k in range(1, last):
+            slots_to(row_cols[k], k)
+
+    low = z < cols // 2
+    high = z >= cols // 2
+    if paired:
+        pl.when(z == 0)(near_part)
+    if row_cols:
+        slots_to(row_cols[0], 0)
+        whole_part(row_cols[0], 0)
+    if paired:
+        pl.when(high)(later_slots)
+        pl.when(z > 0)(near_part)
+    share()
+    if paired:
+        pl.when(low)(later_slots)
+    else:
+        later_slots()
+    for k in range(1, last):
+        whole_part(row_cols[k], k)
     if cols > 1:
         drain(sg_in.at[pl.ds(0, cols - 1)], sr)
     mean = jnp.zeros((1, seq), F32)
@@ -337,6 +393,14 @@
     )
     s_copy.wait_recv()
     grad = grad + s_in[...].astype(F32)
+    if paired:
+        grad_v[...] = grad
+        for k, (on, to) in enumerate(askers):
+            @pl.when(on)
+            def _():
+                far_copy(k, to).wait_recv()
+                grad_v[...] = grad_v[...] + far_in[k].astype(F32)
+        grad = grad_v[...]
     for i, c in enumerate(col_peers):
         drain(p_in.at[c], pr.at[c])
         grad = grad + p_in[c].astype(F32)
@@ -438,9 +502,15 @@
     def kv_copy(to):
         return send(kv_send.at[to], kv_in.at[h], KVS, kvr, {"head": to})
 
-    for r in range(0, rows_w, tile):
-        ctx[:, r : r + tile] = ctx[:, r : r + tile] + product(p, block, r)
-    for r in range(0, rows_w, group):
+    def finish(r):
+        for t in range(r, r + group, min(tile, group)):
+            size = min(tile, group)
+            a, at, depth = block
+            ctx[:, t : t + size] = ctx[:, t : t + size] + mm(
+                a, w_v[p, t : t + size, at : at + depth], NT
+            )
+
+    def back(r):
         part = ctx[:, r : r + group]
         ctx_s = stacked((part[:seq] - taken * part[seq:]).astype(BF16))
         first = r // HEAD_WIDTH
@@ -453,10 +523,23 @@
             for i in range(per):
                 s = i * seq + d * tok
                 q_send[d, :, r + i * HEAD_WIDTH : r + (i + 1) * HEAD_WIDTH] = gq[s : s + tok]
+        return score_grads, probs.astype(BF16), ctx_s
+
+    def depart(r):
         for to in head_peers:
             q_copy(r, to).start()
+
+    groups = list(range(0, rows_w, group))
+    kept = []
+    finish(groups[0])
+    for i, r in enumerate(groups):
+        kept.append(back(r))
+        if i + 1 < len(groups):
+            finish(groups[i + 1])
+        depart(r)
+    for r, (score_grads, probs, ctx_s) in zip(groups, kept):
         gk = gk + mm(score_grads, stacked(q_ref[:, r : r + group]), TN)
-        gv = gv + mm(probs.astype(BF16), ctx_s, TN)
+        gv = gv + mm(probs, ctx_s, TN)
     for d in range(n_head):
         kv_send[d, 0] = gk[d * tok : (d + 1) * tok].astype(BF16)
         kv_send[d, 1] = gv[d * tok : (d + 1) * tok].astype(BF16)
@@ -472,10 +555,16 @@
     others = pl.ds(0, n_head - 1)
     some_cols = pl.ds(0, cols - 1)
     sent = []
+    if row_cols:
+        sent += [(row_send.at[pl.ds(0, len(row_cols))], ROWS)]
+    if paired:
+        far_copy(edge, near).wait_send()
+        for k, (on, to) in enumerate(askers):
+            @pl.when(on)
+            def _():
+                diag_copy(k, to).wait_send()
     if cols > 1:
-        sent += [
-            (row_send.at[some_cols], ROWS),
-            (gt.at[some_cols], GATE), (p_out.at[some_cols], PART), (sg_out.at[some_cols], SLOT)]
+        sent += [(gt.at[some_cols], GATE), (p_out.at[some_cols], PART), (sg_out.at[some_cols], SLOT)]
     if n_head > 1:
         sent += [
             (logit.at[others], LOGIT), (x_all.at[others], XALL), (gh_all.at[others], GH),
@@ -579,9 +668,13 @@
                 vm((n_head, 2, tok, HEAD_WIDTH), BF16),
                 vm((local, seq), F32), vm((local, seq), F32),
                 vm((seq, width), BF16), vm((seq, width), BF16),
-                dma, dma((13,)), dma((cols,)), dma, dma, dma((cols,)), dma((cols,)), dma,
-                dma, dma((n_head, 2)), dma, dma, dma, dma, dma,
+                vm((local, seq), F32), vm((2, local, seq), F32),
+                vm((seq, width), BF16), vm((2, seq, width), BF16),
+                vm((max(cols - 1, 1), pair * room, seq), BF16), vm((seq, width), F32),
+                dma, dma((16,)), dma((cols,)), dma, dma, dma((cols,)), dma((cols,)), dma,
+                dma, dma((n_head, 2)), dma, dma, dma, dma, dma, dma, dma((2,)),
                 pltpu.SemaphoreType.REGULAR, pltpu.SemaphoreType.REGULAR,
+                pltpu.SemaphoreType.REGULAR,
             ],
             compiler_params=pltpu.CompilerParams(
                 collective_id=0, has_side_effects=True, vmem_limit_bytes=48 * 1024 * 1024

time: 29.7 us -> 28.7 us (0.966)
  Pallas kernels: 28.9 us -> 27.9 us
    pallas_call x1, Pallas kernels: 28.2 us -> 27.2 us  [per_device(): pl.pallas_call(functools.partial(kernel, n_exp, n_head, width_total), nam...]
where the time goes in v3:
time: 28.7 us; the launch traced here: 28.6 us
  Pallas kernels  27.9 us (97%)
  between operations  0.64 us (2%)
    pallas_call x1, Pallas kernels, per_device(): pl.pallas_call(functools.partial(kernel, n_exp, n_head, width_total), nam...  27.2 us
    pallas_call x1, Pallas kernels, per_device(): pl.pallas_call(write_out, name='write_out', out_shape=tuple((jax.ShapeDty...  0.72 us

profile of v3, /device:TPU:25, one launch (start us, length us, event | category | flops | bytes accessed | tf_op | source)
XLA Modules:
  0.0 28.6 jit_solution(7746257004551276089)
XLA Ops:
  0.6 27.2 %moe_attention_backward.1 = (bf16[32,1024]{1,0:T(8,128)(2,1)S(1)}, bf16[8,8192]{1,0:T(8,128)(2,1)S(1)}, bf16[8,512]{1,0:T(8,128)(2,1)S(1)}, bf16[8,512]{1,0:T(8,128)(2,1)S(1)}) custom-call(bf16[32,1024]{1,0:T(8,128)(2,1)} %bitcast.17, f32[1,1024]{1,0:T(1,128)} %bitcast.22, f32[1,32]{1,0:T(1,128)} %scale_hbm.1, bf16[32,1024]{1,0:T(8,128)(2,1)} %bitcast.18, ...), custom_call_target="tpu_custom_call" | custom-call | tf_op jit(solution)/shard_map/moe_attention_backward/pallas_call | solution.py:631
  27.8 0.7 %write_out.1 = (bf16[32,1024]{1,0:T(8,128)(2,1)}, bf16[8,8192]{1,0:T(8,128)(2,1)}, bf16[8,512]{1,0:T(8,128)(2,1)}, bf16[8,512]{1,0:T(8,128)(2,1)}) custom-call(bf16[32,1024]{1,0:T(8,128)(2,1)S(1)} %get-tuple-element.12.refs_0_, bf16[8,8192]{1,0:T(8,128)(2,1)S(1)} %get-tuple-element.13.refs_1_, bf16[8,512]{1,0:T(8,128)(2,1)S(1)} %get-tuple-element.14.refs_2_, ...), custom_call_target="tpu_custom_call" | custom-call | tf_op jit(solution)/shard_map/write_out/pallas_call | solution.py:692

commit v4 on v3

--- a/solution.py
+++ b/solution.py
@@ -27,11 +27,11 @@
     x_hbm, gain_hbm, scale_hbm, og_hbm, router_hbm, ids_hbm, expert_hbm, gg_hbm, proj_ref,
     q_hbm, k_hbm, v_hbm,
     gh_out, gq_out, gk_out, gv_out,
-    gain_ref, scale_ref, og_ref, router_ref, ids_ref, expert_ref, gg_ref,
+    gain_ref, scale_ref, og_ref, router_ref, ids_ref, expert_ref, gg_all,
     q_ref, k_ref, v_ref, in_sem,
-    w_v, row_send, rows, gg_in, logit, gt, gates, p_out, p_in, sg_out, sg_in, diff_v, inner_v, gh_all, x_all,
-    ctx, probs_v, q_send, q_in, kv_send, kv_in, across, across_out, s_out, s_in, diag_in, diag_out, far_out, far_in, spread_v, grad_v,
-    w_sem, send_sem, xr, ggr, lr, gr, pr, sr, inr, hr, xar, qr, kvr, acr, shr, dgr, fr, up_sem, down_sem, side_sem,
+    w_v, row_send, rows, logit, gt, gates, p_out, p_in, inner_v, gh_all, x_all,
+    ctx, probs_v, q_send, q_in, kv_send, kv_in, across, across_out, s_out, s_in, diag_in, diag_out, far_out, far_in, near_in, spread_v, grad_v,
+    w_sem, send_sem, xr, ggr, lr, gr, pr, ggzr, inr, hr, xar, qr, kvr, acr, shr, dgr, fr, nr, up_sem, down_sem, side_sem,
 ):
     e = lax.axis_index("exp")
     h = lax.axis_index("head")
@@ -47,7 +47,7 @@
     tok = seq // n_head
     half = width // 2
     partner = 2 * z + 1 - x
-    ROWS, GG, LOGIT, GATE, PART, SLOT, GH, INNER, XALL, QS, KVS, ACROSS, SHARE, FAR, DIAG = range(15)
+    ROWS, GG, LOGIT, GATE, PART, GGZ, GH, INNER, XALL, QS, KVS, ACROSS, SHARE, FAR, NEAR, DIAG = range(16)
 
     def exp_peer(i):
         return {"exp": 2 * i + x}
@@ -99,7 +99,7 @@
     loads = {}
     for i, (name, src, dst) in enumerate((
         ("expert", expert_hbm, expert_ref), ("x", x_hbm, x_all.at[h]), ("gain", gain_hbm, gain_ref),
-        ("router", router_hbm, router_ref), ("gg", gg_hbm, gg_ref), ("ids", ids_hbm, ids_ref),
+        ("router", router_hbm, router_ref), ("gg", gg_hbm, gg_all.at[z, x]), ("ids", ids_hbm, ids_ref),
         ("q", q_hbm, q_ref), ("k", k_hbm, k_ref), ("v", v_hbm, v_ref), ("og", og_hbm, og_ref),
         ("scale", scale_hbm, scale_ref),
     )):
@@ -146,7 +146,7 @@
     pick_all(1 - x, lambda c: row_send.at[c])
     loads["gg"].wait()
     pl.semaphore_wait(barrier, greeted)
-    gg_copy = send(gg_ref, gg_in, GG, ggr, {"exp": partner})
+    gg_copy = send(gg_all.at[z, x], gg_all.at[z, x], GG, ggr, {"exp": partner})
     gg_copy.start()
     for c, j in row_order[:held]:
         row_copy(c, j).start()
@@ -184,6 +184,12 @@
         cp.start()
 
     pick_all(x, lambda c: rows.at[c, 0])
+
+    def near_copy(k, to):
+        return send(rows.at[to, 0], near_in.at[k], NEAR, nr.at[k], exp_peer(to))
+
+    if paired:
+        near_copy(edge, near).start()
 
     if paired:
         pl.semaphore_wait(side_sem, 1)
@@ -216,6 +222,7 @@
     scores = jnp.where(causal, scores, -jnp.inf)
     probs = jnp.exp(scores - jnp.max(scores, axis=1, keepdims=True))
     probs_v[...] = probs / jnp.sum(probs, axis=1, keepdims=True)
+    ctx[...] = jnp.zeros_like(ctx)
 
     expert_i = lax.broadcasted_iota(jnp.int32, (experts_all, seq), 0)
     member = ids_ref[0:1] == expert_i
@@ -286,8 +293,9 @@
 
     earlier = (row_i < col_i).astype(BF16)
     slot_i = lax.broadcasted_iota(jnp.int32, (room, seq), 0)
-    seq_i = lax.broadcasted_iota(jnp.int32, (n_exp, seq), 0)
     gg_copy.wait_recv()
+    for c in col_peers:
+        send(gg_all.at[z], gg_all.at[z], GGZ, ggzr, exp_peer(c)).start()
 
     def places(w):
         named = w >= 0.0
@@ -298,29 +306,22 @@
         spread = [jnp.where(hit, w[j : j + 1], 0.0).astype(BF16) for j, hit in enumerate(hits)]
         return spread, hits
 
-    def contribution(c, w, into):
-        spread, hits = places(jnp.concatenate(by_side(w), axis=0))
-        slots = []
-        for j in range(pair):
-            table = (gg_ref if j < local else gg_in)[j % local]
-            by_seq = mm(table, jnp.where(hits[j][:cap], 1.0, 0.0).astype(BF16))
-            slots.append(
-                jnp.sum(jnp.where(seq_i == 2 * c + x, by_seq, 0.0), axis=0, keepdims=True)
-            )
-        for j in range(pair):
-            into[c, j : j + 1] = jnp.where(x == 0, slots[j], slots[(j + local) % pair])
-        return jnp.concatenate(spread, axis=0)
+    def spreads(w):
+        return jnp.concatenate(places(jnp.concatenate(by_side(w), axis=0))[0], axis=0)
 
     def row_wait(c):
         drain(rows.at[c, 1], xr.at[c])
 
     s_copy = send(s_out, s_in, SHARE, shr, {"exp": partner})
 
+    def share_far():
+        diag_copy(0, near).wait_recv()
+        far_out[...] = shared(diag_in[...], near)
+        far_copy(edge, near).start()
+
     def share():
         if paired:
-            diag_copy(0, near).wait_recv()
-            far_out[...] = shared(diag_in[...], near)
-            far_copy(edge, near).start()
+            share_far()
         across_copy.wait_recv()
         s_out[...] = shared(across[...], z)
         s_copy.start()
@@ -328,15 +329,11 @@
     def part_copy(c):
         return send(p_out.at[c], p_in.at[z], PART, pr.at[z], exp_peer(c))
 
-    def slot_copy(c):
-        return send(sg_out.at[c], sg_in.at[z], SLOT, sr, exp_peer(c))
-
-    spread_z = contribution(z, gt[z], sg_in)
-    grad = mm(spread_z[: local * room], rows[z, 0], TN)
+    spread_z = spreads(gt[z])
+    grad_v[...] = mm(spread_z[: local * room], rows[z, 0], TN)
     def slots_to(c, k):
         gate_wait(c).wait_recv()
-        spread_v[k] = contribution(c, gates[c], sg_out)
-        slot_copy(c).start()
+        spread_v[k] = spreads(gates[c])
 
     def shared(w, c):
         return mm(jnp.concatenate(places(w)[0], axis=0), row_send[c], TN).astype(BF16)
@@ -348,25 +345,17 @@
 
     last = len(row_cols)
 
-    def near_part():
-        slots_to(near, last)
-        p_out[near] = mm(spread_v[last][: local * room], rows[near, 0], TN).astype(BF16)
-        part_copy(near).start()
-
     def later_slots():
         for k in range(1, last):
             slots_to(row_cols[k], k)
 
     low = z < cols // 2
     high = z >= cols // 2
-    if paired:
-        pl.when(z == 0)(near_part)
     if row_cols:
         slots_to(row_cols[0], 0)
         whole_part(row_cols[0], 0)
     if paired:
         pl.when(high)(later_slots)
-        pl.when(z > 0)(near_part)
     share()
     if paired:
         pl.when(low)(later_slots)
@@ -374,23 +363,75 @@
         later_slots()
     for k in range(1, last):
         whole_part(row_cols[k], k)
+    if paired:
+        for k, (on, c) in enumerate(askers):
+            @pl.when(on)
+            def _():
+                near_copy(k, c).wait_recv()
+                spread = jnp.concatenate(places(by_side(gt[c])[0])[0], axis=0)
+                grad_v[...] = grad_v[...] + mm(spread, near_in[k], TN)
     if cols > 1:
-        drain(sg_in.at[pl.ds(0, cols - 1)], sr)
-    mean = jnp.zeros((1, seq), F32)
-    for c in range(cols):
-        mean = mean + jnp.sum(jnp.maximum(gt[c], 0.0) * sg_in[c], axis=0, keepdims=True)
-    for c in range(cols):
-        diff_v[c * pair : (c + 1) * pair] = jnp.maximum(gt[c], 0.0) * (sg_in[c] - mean)
-    diff = diff_v[...]
+        drain(gg_all.at[pl.ds(0, cols - 1)], ggzr)
+    every = jnp.where(member, 1.0, 0.0).astype(BF16)
+    order = mm(every, earlier).astype(jnp.int32)
+    pick_e = lax.broadcasted_iota(jnp.int32, (experts_all, experts_all * n_exp), 0)
+    pick_s = lax.broadcasted_iota(jnp.int32, (experts_all, experts_all * n_exp), 1)
+    own_seq = jnp.where(pick_e * n_exp + e == pick_s, 1.0, 0.0).astype(BF16)
+    table = mm(own_seq, gg_all[...].reshape(experts_all * n_exp, cap))
+    slot_grads = jnp.zeros((experts_all, seq), F32)
+    for s in range(cap):
+        slot_grads = slot_grads + jnp.where(order == s, table[:, s : s + 1], 0.0)
+    weights = jnp.concatenate([jnp.maximum(gt[c], 0.0) for c in range(cols)], axis=0)
+    mean = jnp.sum(weights * slot_grads, axis=0, keepdims=True)
+    diff = weights * (slot_grads - mean)
     diff_hi = diff.astype(BF16)
     diff_lo = (diff - diff_hi.astype(F32)).astype(BF16)
-    grad = grad + mm(diff_hi, router_ref[...], TN) + mm(diff_lo, router_ref[...], TN)
+    grad = grad_v[...] + mm(diff_hi, router_ref[...], TN) + mm(diff_lo, router_ref[...], TN)
     loads["og"].wait()
     loads["scale"].wait()
     scale = jnp.sum(
         jnp.where(row_i == col_i, jnp.broadcast_to(scale_ref[...], (seq, seq)), 0.0),
         axis=1, keepdims=True,
     )
+    rows_w = w_v.shape[1]
+    tile = min(512, rows_w)
+    group = max(rows_w // 2, HEAD_WIDTH)
+    per = group // HEAD_WIDTH
+
+    def piece(p, k):
+        return (
+            jnp.concatenate([gh_all[p, k], x_all[p, :, k * half : (k + 1) * half]], axis=0),
+            k * half, half,
+        )
+
+    def whole(p):
+        return (
+            jnp.concatenate(
+                [jnp.concatenate([gh_all[p, 0], gh_all[p, 1]], axis=1), x_all[p]], axis=0
+            ),
+            0, width,
+        )
+
+    def product(p, block, r):
+        a, at, size = block
+        return mm(a, w_v[p, r : r + tile, at : at + size], NT)
+
+    def add_product(p, block):
+        for r in range(0, rows_w, tile):
+            ctx[:, r : r + tile] = ctx[:, r : r + tile] + product(p, block, r)
+
+    def arrived(p, k):
+        for kk in (0, 1) if k is None else (k,):
+            drain(gh_all.at[p, kk], hr.at[p, kk])
+
+    def stage(p, k):
+        arrived(p, k)
+        add_product(p, whole(p) if k is None else piece(p, k))
+
+    drain(w_v, w_sem)
+    if n_head > 1:
+        drain(x_all.at[pl.ds(0, n_head - 1)], xar)
+
     s_copy.wait_recv()
     grad = grad + s_in[...].astype(F32)
     if paired:
@@ -401,9 +442,16 @@
                 far_copy(k, to).wait_recv()
                 grad_v[...] = grad_v[...] + far_in[k].astype(F32)
         grad = grad_v[...]
-    for i, c in enumerate(col_peers):
-        drain(p_in.at[c], pr.at[c])
-        grad = grad + p_in[c].astype(F32)
+    if row_cols:
+        grad_v[...] = grad
+        for c in range(cols):
+            beside = c + 1 if c < cols - 1 else c - 1
+
+            @pl.when(jnp.logical_and(z != c, z != beside))
+            def _():
+                drain(p_in.at[c], pr.at[c])
+                grad_v[...] = grad_v[...] + p_in[c].astype(F32)
+        grad = grad_v[...]
 
 
     def gh_copy(src, k, to):
@@ -413,6 +461,9 @@
 
     def half_of(a, k):
         return a[:, k * half : (k + 1) * half]
+
+    def inner_copy(src, to):
+        return send(inner_v.at[src], inner_v.at[src], INNER, inr, {"head": to})
 
     base = []
     for k in range(2):
@@ -422,58 +473,25 @@
         gh_all[h, k] = base[k].astype(BF16)
         for p in [sibling] + same:
             gh_copy(h, k, p).start()
-    for p in cross:
-        for k in range(2):
+        if k == 0:
+            inner_v[h] = jnp.broadcast_to(
+                jnp.sum(hidden_f32() * gain * grad, axis=1, keepdims=True), (seq, HEAD_WIDTH)
+            )
+            for p in head_peers:
+                inner_copy(h, p).start()
+    for k in range(2):
+        for p in cross:
             gh_copy(h, k, p).start()
-    inner_v[h] = jnp.broadcast_to(
-        jnp.sum(hidden_f32() * gain * grad, axis=1, keepdims=True), (seq, HEAD_WIDTH)
-    )
-
-    def inner_copy(src, to):
-        return send(inner_v.at[src], inner_v.at[src], INNER, inr, {"head": to})
-
-    for p in head_peers:
-        inner_copy(h, p).start()
-    drain(w_v, w_sem)
-    if n_head > 1:
-        drain(x_all.at[pl.ds(0, n_head - 1)], xar)
-
-    rows_w = w_v.shape[1]
-    tile = min(512, rows_w)
-    group = max(rows_w // 2, HEAD_WIDTH)
-    per = group // HEAD_WIDTH
-
-    def piece(p, k):
-        return (
-            jnp.concatenate([gh_all[p, k], x_all[p, :, k * half : (k + 1) * half]], axis=0),
-            k * half, half,
-        )
-
-    def whole(p):
-        return (
-            jnp.concatenate(
-                [jnp.concatenate([gh_all[p, 0], gh_all[p, 1]], axis=1), x_all[p]], axis=0
-            ),
-            0, width,
-        )
-
-    def product(p, block, r):
-        a, at, size = block
-        return mm(a, w_v[p, r : r + tile, at : at + size], NT)
-
-    stages = [(h, None)] + [(sibling, None)]
-    for p in same + cross:
-        stages += [(p, 0), (p, 1)]
+    add_product(h, whole(h))
+    if chips > 1:
+        stages = [(sibling, None)]
+        for p in same + cross:
+            stages += [(p, 0), (p, 1)]
+    else:
+        stages = [(sibling, None)]
     for i, (p, k) in enumerate(stages[:-1]):
-        if i:
-            for kk in (0, 1) if k is None else (k,):
-                drain(gh_all.at[p, kk], hr.at[p, kk])
-        block = whole(p) if k is None else piece(p, k)
-        for r in range(0, rows_w, tile):
-            part = product(p, block, r)
-            if i:
-                part = ctx[:, r : r + tile] + part
-            ctx[:, r : r + tile] = part
+        arrived(p, k)
+        add_product(p, whole(p) if k is None else piece(p, k))
 
     if n_head > 1:
         drain(inner_v.at[pl.ds(0, n_head - 1)], inr)
@@ -483,13 +501,8 @@
     taken = scale * inner[:, 0:1] / width_total
 
     p, k = stages[-1]
-    if k is None:
-        for kk in (0, 1):
-            drain(gh_all.at[p, kk], hr.at[p, kk])
-        block = whole(p)
-    else:
-        drain(gh_all.at[p, k], hr.at[p, k])
-        block = piece(p, k)
+    arrived(p, k)
+    block = whole(p) if k is None else piece(p, k)
     key_block = k_ref[:, lanes]
     value_block = v_ref[:, lanes]
     gk = jnp.zeros((seq, HEAD_WIDTH), F32)
@@ -556,15 +569,19 @@
     some_cols = pl.ds(0, cols - 1)
     sent = []
     if row_cols:
-        sent += [(row_send.at[pl.ds(0, len(row_cols))], ROWS)]
-    if paired:
+        sent += [
+            (row_send.at[pl.ds(0, len(row_cols))], ROWS), (p_out.at[pl.ds(0, len(row_cols))], PART),
+        ]
+    if paired:
+        near_copy(edge, near).wait_send()
+        gate_wait(near).wait_recv()
         far_copy(edge, near).wait_send()
         for k, (on, to) in enumerate(askers):
             @pl.when(on)
             def _():
                 diag_copy(k, to).wait_send()
     if cols > 1:
-        sent += [(gt.at[some_cols], GATE), (p_out.at[some_cols], PART), (sg_out.at[some_cols], SLOT)]
+        sent += [(gt.at[some_cols], GATE), (gg_all.at[some_cols], GGZ)]
     if n_head > 1:
         sent += [
             (logit.at[others], LOGIT), (x_all.at[others], XALL), (gh_all.at[others], GH),
@@ -643,20 +660,16 @@
                 vm((1, width), F32), vm((1, seq), F32),
                 vm((seq, width), BF16), vm((experts_all, width), BF16),
                 vm((top_k, seq), jnp.int32), vm((local, cap, n_exp, width), BF16),
-                vm(gate_grad.shape, BF16), vm((seq, span), BF16),
+                vm((cols, 2) + gate_grad.shape, BF16), vm((seq, span), BF16),
                 vm((seq, kv_width), BF16), vm((seq, kv_width), BF16), dma((11,)),
                 vm((n_head, span, width), BF16),
                 vm((cols, local * room, width), BF16),
                 vm((cols, 2, local * room, width), BF16),
-                vm(gate_grad.shape, BF16),
                 vm((n_head, experts_all, seq), F32),
                 vm((cols, pair, seq), F32),
                 vm((cols, pair, seq), F32),
                 vm((cols, seq, width), BF16),
                 vm((cols, seq, width), BF16),
-                vm((cols, pair, seq), F32),
-                vm((cols, pair, seq), F32),
-                vm((experts_all, seq), F32),
                 vm((n_head, seq, HEAD_WIDTH), F32),
                 vm((n_head, 2, seq, width // 2), BF16),
                 vm((n_head, seq, width), BF16),
@@ -670,9 +683,10 @@
                 vm((seq, width), BF16), vm((seq, width), BF16),
                 vm((local, seq), F32), vm((2, local, seq), F32),
                 vm((seq, width), BF16), vm((2, seq, width), BF16),
+                vm((2, local * room, width), BF16),
                 vm((max(cols - 1, 1), pair * room, seq), BF16), vm((seq, width), F32),
-                dma, dma((16,)), dma((cols,)), dma, dma, dma((cols,)), dma((cols,)), dma,
-                dma, dma((n_head, 2)), dma, dma, dma, dma, dma, dma, dma((2,)),
+                dma, dma((17,)), dma((cols,)), dma, dma, dma((cols,)), dma((cols,)), dma,
+                dma, dma((n_head, 2)), dma, dma, dma, dma, dma, dma, dma((2,)), dma((2,)),
                 pltpu.SemaphoreType.REGULAR, pltpu.SemaphoreType.REGULAR,
                 pltpu.SemaphoreType.REGULAR,
             ],

time: 28.7 us -> 28.2 us (0.983)
  Pallas kernels: 27.9 us -> 27.2 us
    pallas_call x1, Pallas kernels: 27.2 us -> 26.5 us  [per_device(): pl.pallas_call(functools.partial(kernel, n_exp, n_head, width_total), nam...]
where the time goes in v4:
time: 28.2 us; the launch traced here: 27.8 us
  Pallas kernels  27.2 us (96%)
  between operations  0.64 us (2%)
    pallas_call x1, Pallas kernels, per_device(): pl.pallas_call(functools.partial(kernel, n_exp, n_head, width_total), nam...  26.5 us
    pallas_call x1, Pallas kernels, per_device(): pl.pallas_call(write_out, name='write_out', out_shape=tuple((jax.ShapeDty...  0.72 us

profile of v4, /device:TPU:25, one launch (start us, length us, event | category | flops | bytes accessed | tf_op | source)
XLA Modules:
  0.0 27.8 jit_solution(16232744029409994179)
XLA Ops:
  0.6 26.5 %moe_attention_backward.1 = (bf16[32,1024]{1,0:T(8,128)(2,1)S(1)}, bf16[8,8192]{1,0:T(8,128)(2,1)S(1)}, bf16[8,512]{1,0:T(8,128)(2,1)S(1)}, bf16[8,512]{1,0:T(8,128)(2,1)S(1)}) custom-call(bf16[32,1024]{1,0:T(8,128)(2,1)} %bitcast.17, f32[1,1024]{1,0:T(1,128)} %bitcast.22, f32[1,32]{1,0:T(1,128)} %scale_hbm.1, bf16[32,1024]{1,0:T(8,128)(2,1)} %bitcast.18, ...), custom_call_target="tpu_custom_call" | custom-call | tf_op jit(solution)/shard_map/moe_attention_backward/pallas_call | solution.py:648
  27.1 0.7 %write_out.1 = (bf16[32,1024]{1,0:T(8,128)(2,1)}, bf16[8,8192]{1,0:T(8,128)(2,1)}, bf16[8,512]{1,0:T(8,128)(2,1)}, bf16[8,512]{1,0:T(8,128)(2,1)}) custom-call(bf16[32,1024]{1,0:T(8,128)(2,1)S(1)} %get-tuple-element.12.refs_0_, bf16[8,8192]{1,0:T(8,128)(2,1)S(1)} %get-tuple-element.13.refs_1_, bf16[8,512]{1,0:T(8,128)(2,1)S(1)} %get-tuple-element.14.refs_2_, ...), custom_call_target="tpu_custom_call" | custom-call | tf_op jit(solution)/shard_map/write_out/pallas_call | solution.py:706
